TPU v7x, 128 devices: a whole 4x4x4 slice. The times are simulated.
128 devices in a mesh: dp: 16 (over x, y), vocab: 8 (over z, core).
Axes of the slice: x: 4, y: 4, z: 4, core: 2. Of those that a mesh axis runs over, the one named last changes fastest.
Arguments:
- hidden: bfloat16 [768, 8192], P('dp', 'vocab'), may hold values from -32 to 32
- head_weight: bfloat16 [8192, 128256], P(None, ('dp', 'vocab')), may hold values from -0.9943689 to 0.9943689
- critic_in: bfloat16 [16, 8192, 4096], P('dp', None, 'vocab'), may hold values from -0.0625 to 0.0625
- critic_out: bfloat16 [16, 4096], P('dp', 'vocab'), may hold values from -0.09375 to 0.09375
- rewards: float32 [16, 12], P('dp'), may hold values from -4 to 4
- turn_ids: int32 [16, 48], P('dp'), may hold values from 0 to 11, never falling along the last dimension, each value on 1 to 8 neighbouring positions
- owners: int32 [192, 1], P('dp'), may hold values from 0 to 15; in each aligned block of 12 rows (0 to 11, 12 to 23, ...) at most 2 rows name the same one
- actions: int32 [768], replicated, may hold values from 0 to 128255
Outputs:
- hidden_grad: float32 [768, 8192], P('dp', 'vocab')
- token_logprob: float32 [768], P('dp')
- turn_advantage: float32 [16, 12], P('dp')
Inputs may be any that keep to these rules, and one draw needn't show every extreme that they name: `turn_ids`: in each row, turn numbers never fall, every number of 0 to 11 appears, and each turn has 1 to 8 tokens. `owners`: among the 12 turns of one index of dp, at most 2 name the same critic, and every critic is named by some turn.
All inputs are finite; a program needn't handle non-finite values.
Results may differ from a plain program's by a relative error of at most 0.0087.
Values may be sent and summed in bfloat16 or wider, within the bound.
No kernel may reach another device: no remote copies, remote signals or barrier semaphores. Data moves between devices by JAX's collectives and lax.ppermute only.
A program may use at most 128 MiB of HBM per device.

v0:
```python
import jax
import jax.numpy as jnp
from jax import lax
from jax.sharding import Mesh
from jax.sharding import PartitionSpec as P

DP = ("dp_0", "dp_1")
VOCAB = ("vocab_0", "vocab_1")
DP_VOCAB = ("dp_0", "dp_1", "vocab_0", "vocab_1")


epsilon = 1e-05
loss_scale = 32.0


def sent_to_all(x, axis):
    size = lax.axis_size(axis)
    return lax.all_to_all(jnp.broadcast_to(x[None], (size, *x.shape)), axis, 0, 0, tiled=True)


def in_order(parts, dim):
    parts = jnp.moveaxis(parts, 0, dim)
    shape = parts.shape
    return parts.reshape(*shape[:dim], shape[dim] * shape[dim + 1], *shape[dim + 2 :])


def gather_directly(x, axis, dim):
    parts = sent_to_all(x, axis)
    return in_order(parts, dim)


def over_copies(x, axis):
    return sent_to_all(x, axis).sum(axis=0)


def all_in_one(x, axis):
    leaves = jax.tree.leaves(x)
    order = sorted(range(len(leaves)), key=lambda k: -leaves[k].size)
    width = (1, *leaves[order[0]].shape)[-1]
    lines = [
        jnp.pad(leaves[k].reshape(-1), (0, -leaves[k].size % width)).reshape(-1, width)
        for k in order
    ]
    both, at, found = (lax.all_gather(jnp.concatenate(lines), axis), 0, {})
    for k, line in zip(order, lines):
        slab = both[:, at : at + len(line)].reshape(len(both), -1)
        found[k] = slab[:, : leaves[k].size].reshape(-1, *leaves[k].shape)
        at += len(line)
    numbers = iter(range(len(leaves)))
    return jax.tree.map(lambda _: found[next(numbers)], x)


def merged_by_axis(x, axes, combine):
    for axis in axes:
        pieces = all_in_one(x, axis)
        x = jax.tree.map(lambda part: part[0], pieces)
        for k in range(1, lax.axis_size(axis)):
            x = combine(x, jax.tree.map(lambda part: part[k], pieces))
    return x


def in_blocks(x, dim, size):
    before, after = (x.shape[:dim], x.shape[dim + 1 :])
    return jnp.moveaxis(x.reshape(*before, size, -1, *after), dim, 0)


def summed_on_arrival(x, axis, dim):
    size = lax.axis_size(axis)
    parts = lax.all_to_all(in_blocks(x, dim, size), axis, 0, 0, tiled=True)
    return jnp.sum(parts.astype(jnp.float32), axis=0)


def rms_norm(values):
    return values * lax.rsqrt(jnp.mean(values * values, axis=-1, keepdims=True) + epsilon)


def combine_rows(left_stats, right_stats):
    joint_top = jnp.maximum(left_stats[0], right_stats[0])
    joint_mass = left_stats[1] * jnp.exp(left_stats[0] - joint_top) + right_stats[1] * jnp.exp(
        right_stats[0] - joint_top
    )
    return (joint_top, joint_mass, left_stats[2] + right_stats[2])


def on_device(hidden, head_weight, critic_in, critic_out, rewards, turn_ids, owners, actions):
    ranks_dp = lax.axis_size(DP)
    ranks_vocab = lax.axis_size(VOCAB)
    tok_dev = hidden.shape[0]
    turn_dev = rewards.shape[1]
    slot_count = max(2, 2 * turn_dev // ranks_dp)
    vocab_local = head_weight.shape[1]
    feats = gather_directly(hidden, VOCAB, 1)
    position = jnp.arange(tok_dev, dtype=jnp.int32)
    turn_range = jnp.arange(turn_dev, dtype=jnp.int32)
    member = turn_ids[0][None, :] == turn_range[:, None]
    last_pos = jnp.max(jnp.where(member, position[None, :], -1), axis=1)
    end_pick = (position[None, :] == last_pos[:, None]).astype(jnp.bfloat16)
    owner_of = owners[:, 0]
    earlier = (owner_of[None, :] == owner_of[:, None]) & (turn_range[None, :] < turn_range[:, None])
    slot_of = jnp.sum(earlier.astype(jnp.int32), axis=1)
    dest_range = jnp.arange(ranks_dp, dtype=jnp.int32)
    slot_range = jnp.arange(slot_count, dtype=jnp.int32)
    dispatch = (owner_of[:, None, None] == dest_range[None, :, None]) & (
        slot_of[:, None, None] == slot_range[None, None, :]
    )
    route_matrix = dispatch.reshape(turn_dev, ranks_dp * slot_count).astype(jnp.bfloat16)
    end_slices = jnp.dot(end_pick, hidden, preferred_element_type=jnp.float32).astype(jnp.bfloat16)
    outgoing = jnp.dot(route_matrix.T, end_slices, preferred_element_type=jnp.float32).astype(
        jnp.bfloat16
    )
    outgoing = outgoing.reshape(ranks_dp, slot_count, hidden.shape[1])
    whole_rows = gather_directly(
        lax.all_to_all(outgoing, DP, split_axis=0, concat_axis=0, tiled=True), VOCAB, 2
    )
    flat_rows = whole_rows.reshape(-1, whole_rows.shape[2]).astype(jnp.float32)
    normed = rms_norm(flat_rows).astype(jnp.bfloat16)
    inner = jnp.dot(normed, critic_in[0], preferred_element_type=jnp.float32)
    active = jax.nn.silu(inner).astype(jnp.bfloat16)
    partial_value = jnp.dot(active, critic_out[0], preferred_element_type=jnp.float32)
    summed_value = over_copies(partial_value, VOCAB)
    values = lax.all_to_all(
        summed_value.reshape(whole_rows.shape[0], whole_rows.shape[1]),
        DP,
        split_axis=0,
        concat_axis=0,
        tiled=True,
    )
    turn_value = jnp.sum(jnp.where(dispatch, values[None, :, :], 0.0), axis=(1, 2))
    advantage = rewards[0] - turn_value
    token_adv = jnp.sum(jnp.where(member, advantage[:, None], 0.0), axis=0)
    token_adv_all = gather_directly(token_adv, DP, 0)
    logits = jnp.dot(
        lax.all_gather(feats, DP, axis=0, tiled=True),
        head_weight,
        preferred_element_type=jnp.float32,
    )
    first_col = (lax.axis_index(DP) * ranks_vocab + lax.axis_index(VOCAB)) * vocab_local
    local_action = actions - first_col
    hit = jnp.arange(vocab_local, dtype=jnp.int32)[None, :] == local_action[:, None]
    picked_part = jnp.sum(jnp.where(hit, logits, 0.0), axis=1)
    local_top = jnp.max(logits, axis=1)
    local_mass = jnp.sum(jnp.exp(logits - local_top[:, None]), axis=1)
    row_top, row_mass, picked = merged_by_axis(
        (local_top, local_mass, picked_part), DP_VOCAB, combine_rows
    )
    logprob_all = picked - row_top - jnp.log(row_mass)
    token_logprob = lax.dynamic_slice_in_dim(logprob_all, lax.axis_index(DP) * tok_dev, tok_dev, 0)
    probs = jnp.exp(logits - row_top[:, None]) / row_mass[:, None]
    grad_logits = (loss_scale * token_adv_all[:, None] * (probs - hit.astype(jnp.float32))).astype(
        jnp.bfloat16
    )
    summed = lax.psum_scatter(
        lax.dot_general(
            head_weight, grad_logits, (((1,), (1,)), ((), ())), preferred_element_type=jnp.float32
        ).astype(jnp.bfloat16),
        VOCAB,
        scatter_dimension=0,
        tiled=True,
    )
    hidden_grad = summed_on_arrival(summed, DP, 1).T
    return (hidden_grad, token_logprob, advantage[None, :])


def solution(mesh):
    finer = Mesh(mesh.devices.reshape(4, 4, 4, 2), ("dp_0", "dp_1", "vocab_0", "vocab_1"))
    return jax.shard_map(
        on_device,
        mesh=finer,
        in_specs=(
            P(DP, VOCAB),
            P(None, DP_VOCAB),
            P(DP, None, VOCAB),
            P(DP, VOCAB),
            P(DP, None),
            P(DP, None),
            P(DP, None),
            P(),
        ),
        out_specs=(P(DP, VOCAB), P(DP), P(DP, None)),
        check_vma=False,
    )
```

profile of v0, /device:TPU:0, one launch (start us, length us, event | category | flops | bytes accessed | tf_op | source)
XLA Modules:
  0.0 306.4 jit_solution(6042084861229372551)
XLA Ops:
  7.2 0.0 copy-start
  7.2 0.0 all-gather.10.cloned.1.call-start
  7.3 1.0 broadcast_in_dim.57
  8.2 18.4 %all_to_all.41 = bf16[8,48,1024]{2,1,0:T(8,128)(2,1)S(1)} all-to-all(bf16[8,48,1024]{2,1,0:T(8,128)(2,1)S(1)} %broadcast_in_dim.57), channel_id=1, replica_groups=mesh['dp_0'=4,'dp_1'=4,'vocab_0'=4,'vocab_1'=2] {'vocab_0','vocab_1'}, dimensions={0} | all-to-all | bytes 1572864 | tf_op jit(solution)/shard_map/all_to_all | solution.py:18
  26.6 1.0 copy.32
  27.6 0.0 all-gather.10.cloned.1.call-update
  27.7 0.2 convert_reduce_fusion.1
  27.9 0.1 select_reduce_fusion.3
  28.0 0.3 convolution_convert_fusion.1
  28.4 14.5 %all_to_all.42 = bf16[16,2,1024]{2,1,0:T(2,128)(2,1)S(1)} all-to-all(bf16[16,2,1024]{2,1,0:T(2,128)(2,1)S(1)} %reshape.901), channel_id=1, replica_groups=mesh['dp_0'=4,'dp_1'=4,'vocab_0'=4,'vocab_1'=2] {'dp_0','dp_1'}, dimensions={0} | all-to-all | bytes 131072 | tf_op jit(solution)/shard_map/all_to_all | solution.py:113
  42.9 1.1 broadcast_in_dim.48
  44.0 3.5 %all-to-all-start.1 = ((bf16[8,16,2,1024]{3,2,1,0:T(2,128)(2,1)}), bf16[8,16,2,1024]{3,2,1,0:T(2,128)(2,1)S(1)}, u32[]{:S(2)}, u32[]{:S(2)}) async-start(bf16[8,16,2,1024]{3,2,1,0:T(2,128)(2,1)} %broadcast_in_dim.48), calls=%async_computation.1 | async-start | bytes 1048576 | tf_op jit(solution)/shard_map/all_to_all | solution.py:18
  47.5 10.2 %all-to-all-done.1 = bf16[8,16,2,1024]{3,2,1,0:T(2,128)(2,1)S(1)} async-done(((bf16[8,16,2,1024]{3,2,1,0:T(2,128)(2,1)}), bf16[8,16,2,1024]{3,2,1,0:T(2,128)(2,1)S(1)}, u32[]{:S(2)}, u32[]{:S(2)}) %all-to-all-start.1) | async-done | bytes 524320 | tf_op jit(solution)/shard_map/all_to_all | solution.py:18
  57.7 0.6 fusion.7
  58.4 0.5 fusion.9
  58.9 0.3 copy.25
  59.2 0.3 copy.33
  59.5 0.0 copy-start.5
  59.5 0.0 copy-start.2
  59.6 5.1 %convolution_bitcast_fusion = f32[32]{0:T(128)S(1)} fusion(bf16[32,8192]{1,0:T(8,128)(2,1)S(1)} %bitcast.275, bf16[1,8192,512]{2,1,0:T(8,128)(2,1)} %param.10, bf16[1,512]{1,0:T(2,128)(2,1)S(1)} %copy-done), kind=kOutput, calls=%fused_computation.17 | convolution fusion | flops 268550144 | bytes 8914048 | tf_op jit(solution)/shard_map/dot_general | solution.py:119
  64.6 0.6 broadcast_in_dim.49
  65.2 3.3 %all-to-all-start.2 = ((f32[8,1,32]{2,1,0:T(1,128)}), f32[8,1,32]{2,1,0:T(1,128)S(1)}, u32[]{:S(2)}, u32[]{:S(2)}) async-start(f32[8,1,32]{2,1,0:T(1,128)} %broadcast_in_dim.49), calls=%async_computation.2 | async-start | bytes 8192 | tf_op jit(solution)/shard_map/all_to_all | solution.py:18
  68.6 5.1 %all-to-all-done.2 = f32[8,1,32]{2,1,0:T(1,128)S(1)} async-done(((f32[8,1,32]{2,1,0:T(1,128)}), f32[8,1,32]{2,1,0:T(1,128)S(1)}, u32[]{:S(2)}, u32[]{:S(2)}) %all-to-all-start.2) | async-done | bytes 1056 | tf_op jit(solution)/shard_map/all_to_all | solution.py:18
  73.7 0.7 all_to_all.29
  74.4 3.5 %all-to-all-start.3 = ((f32[16,1,2]{2,1,0:T(1,128)}), f32[16,1,2]{2,1,0:T(1,128)S(1)}, u32[]{:S(2)}, u32[]{:S(2)}) async-start(f32[16,1,2]{2,1,0:T(1,128)} %bitcast.7), calls=%async_computation.3 | async-start | bytes 16384 | tf_op jit(solution)/shard_map/all_to_all | solution.py:121
  77.9 7.6 %all-to-all-done.3 = f32[16,1,2]{2,1,0:T(1,128)S(1)} async-done(((f32[16,1,2]{2,1,0:T(1,128)}), f32[16,1,2]{2,1,0:T(1,128)S(1)}, u32[]{:S(2)}, u32[]{:S(2)}) %all-to-all-start.3) | async-done | bytes 160 | tf_op jit(solution)/shard_map/all_to_all | solution.py:121
  85.5 0.1 select_reduce_fusion.1
  85.6 0.1 select_reduce_fusion.2
  85.7 0.6 broadcast_in_dim.56
  86.3 3.5 %all-to-all-start.4 = ((f32[16,1,48]{2,1,0:T(1,128)}), f32[16,1,48]{2,1,0:T(1,128)S(1)}, u32[]{:S(2)}, u32[]{:S(2)}) async-start(f32[16,1,48]{2,1,0:T(1,128)} %broadcast_in_dim.56), calls=%async_computation.4 | async-start | bytes 16384 | tf_op jit(solution)/shard_map/all_to_all | solution.py:18
  89.8 0.0 reduce-scatter.2.cloned.1.call-start
  89.9 7.5 %all-to-all-done.4 = f32[16,1,48]{2,1,0:T(1,128)S(1)} async-done(((f32[16,1,48]{2,1,0:T(1,128)}), f32[16,1,48]{2,1,0:T(1,128)S(1)}, u32[]{:S(2)}, u32[]{:S(2)}) %all-to-all-start.4) | async-done | bytes 3104 | tf_op jit(solution)/shard_map/all_to_all | solution.py:18
  97.4 0.1 mul.257
  97.5 19.7 %all-gather.10.cloned.1.call-done = bf16[768,8192]{1,0:T(8,128)(2,1)} async-done(((bf16[48,8192]{1,0:T(8,128)(2,1)}), bf16[768,8192]{1,0:T(8,128)(2,1)}) %all-gather.10.cloned.1.call-update) | async-done | bytes 12582928 | tf_op jit(solution)/shard_map/all_gather | solution.py:133
  117.2 18.7 %fusion.63 = (f32[768]{0:T(1024)S(1)}, f32[768,1002]{0,1:T(8,128)S(1)}) fusion(bf16[768,8192]{1,0:T(8,128)(2,1)} %all-gather.10.cloned.1.call-done, bf16[8192,1002]{0,1:T(8,128)(2,1)} %param.9), kind=kOutput, calls=%fused_computation.126 | convolution fusion | flops 12608846848 | bytes 32080896 | tf_op jit(solution)/shard_map/dot_general | solution.py:132
  135.9 0.8 exponential_reduce_fusion
  136.8 12.2 %all-gather.4 = f32[4,3,768]{2,1,0:T(4,128)S(1)} all-gather(f32[1,3,768]{2,1,0:T(4,128)S(1)} %maximum_bitcast_fusion), channel_id=2, replica_groups=mesh['dp_0'=4,'dp_1'=4,'vocab_0'=4,'vocab_1'=2] {'dp_0'}, dimensions={0}, use_global_device_ids=true | all-gather | bytes 46080 | tf_op jit(solution)/shard_map/all_gather | solution.py:44
  149.0 11.9 %all-gather.5 = f32[4,3,768]{2,1,0:T(4,128)S(1)} all-gather(f32[1,3,768]{2,1,0:T(4,128)S(1)} %maximum_bitcast_fusion.1), channel_id=3, replica_groups=mesh['dp_0'=4,'dp_1'=4,'vocab_0'=4,'vocab_1'=2] {'dp_1'}, dimensions={0}, use_global_device_ids=true | all-gather | bytes 46080 | tf_op jit(solution)/shard_map/all_gather | solution.py:44
  161.0 12.4 %all-gather.6 = f32[4,3,768]{2,1,0:T(4,128)S(1)} all-gather(f32[1,3,768]{2,1,0:T(4,128)S(1)} %maximum_bitcast_fusion.2), channel_id=4, replica_groups=mesh['dp_0'=4,'dp_1'=4,'vocab_0'=4,'vocab_1'=2] {'vocab_0'}, dimensions={0}, use_global_device_ids=true | all-gather | bytes 46080 | tf_op jit(solution)/shard_map/all_gather | solution.py:44
  173.5 2.0 all-gather.7
  175.6 21.9 %fusion = bf16[8192,768]{0,1:T(8,128)(2,1)} fusion(bf16[8192,1002]{0,1:T(8,128)(2,1)} %param.9, f32[768,1002]{0,1:T(8,128)S(1)} %get-tuple-element.20, f32[768]{0:T(1024)S(1)} %get-tuple-element.11, f32[768]{0:T(1024)S(1)} %get-tuple-element.12, s32[768]{0:T(1024)S(1)} %broadcast_subtract_fusion, f32[768]{0:T(1024)S(1)} %mul.257), kind=kOutput, calls=%fused_computation.1 | convolution fusion | flops 12619755520 | bytes 32090112 | tf_op jit(solution)/shard_map/dot_general | solution.py:153
  197.5 0.0 reduce-scatter.2.cloned.1.call-update
  197.5 71.2 %reduce-scatter.2.cloned.1.call-done = bf16[1024,768]{0,1:T(8,128)(2,1)} async-done(((bf16[8192,768]{0,1:T(8,128)(2,1)}), bf16[1024,768]{0,1:T(8,128)(2,1)}) %reduce-scatter.2.cloned.1.call-update) | async-done | bytes 1572880 | tf_op jit(solution)/shard_map/reduce_scatter | solution.py:152
  268.7 6.8 %all-to-all-start.6 = ((bf16[16,1024,48]{1,2,0:T(8,128)(2,1)}), bf16[16,1024,48]{1,2,0:T(8,128)(2,1)S(1)}, u32[]{:S(2)}, u32[]{:S(2)}) async-start(bf16[16,1024,48]{1,2,0:T(8,128)(2,1)} %bitcast.277), calls=%async_computation.7 | async-start | bytes 3145728 | tf_op jit(solution)/shard_map/all_to_all | solution.py:69
  275.5 0.5 bitcast_subtract_fusion
  276.0 0.6 dynamic_slice.3
  276.6 22.0 %all-to-all-done.6 = bf16[16,1024,48]{1,2,0:T(8,128)(2,1)S(1)} async-done(((bf16[16,1024,48]{1,2,0:T(8,128)(2,1)}), bf16[16,1024,48]{1,2,0:T(8,128)(2,1)S(1)}, u32[]{:S(2)}, u32[]{:S(2)}) %all-to-all-start.6) | async-done | bytes 1572896 | tf_op jit(solution)/shard_map/all_to_all | solution.py:69
  298.6 1.0 convert_reduce_fusion
  (34 shorter events, 0.5 us)
Async XLA Ops:
  7.2 52.4 %copy-start = (bf16[1,512]{1,0:T(2,128)(2,1)S(1)}, bf16[1,512]{1,0:T(2,128)(2,1)}, u32[]{:S(2)}) copy-start(bf16[1,512]{1,0:T(2,128)(2,1)} %param.11) | copy-start | bytes 3076
  7.2 20.9 %copy-start.1 = (bf16[48,1024]{1,0:T(8,128)(2,1)S(1)}, bf16[48,1024]{1,0:T(8,128)(2,1)}, u32[]{:S(2)}) copy-start(bf16[48,1024]{1,0:T(8,128)(2,1)} %param.8) | copy-start | bytes 294916
  7.2 20.5 %copy-start.3 = (s32[12,1]{0,1:T(1,128)S(1)}, s32[12,1]{0,1:T(1,128)}, u32[]{:S(2)}) copy-start(s32[12,1]{0,1:T(1,128)} %param.14) | copy-start | bytes 148
  7.2 20.7 %copy-start.4 = (s32[1,48]{1,0:T(1,128)S(1)}, s32[1,48]{1,0:T(1,128)}, u32[]{:S(2)}) copy-start(s32[1,48]{1,0:T(1,128)} %param.13) | copy-start | bytes 580
  7.2 110.0 %all-gather.10.cloned.1.call-start = ((), (), s32[]{:S(2)}) async-start(), calls=%async_computation.8 | async-start | bytes 13369344 | tf_op jit(solution)/shard_map/all_gather | solution.py:133
  44.0 13.7 %all-to-all-start.1 = ((bf16[8,16,2,1024]{3,2,1,0:T(2,128)(2,1)}), bf16[8,16,2,1024]{3,2,1,0:T(2,128)(2,1)S(1)}, u32[]{:S(2)}, u32[]{:S(2)}) async-start(bf16[8,16,2,1024]{3,2,1,0:T(2,128)(2,1)} %broadcast_in_dim.48), calls=%async_computation.1 | async-start | bytes 1048576 | tf_op jit(solution)/shard_map/all_to_all | solution.py:18
  59.5 26.1 %copy-start.5 = (f32[1,12]{1,0:T(1,128)S(1)}, f32[1,12]{1,0:T(1,128)}, u32[]{:S(2)}) copy-start(f32[1,12]{1,0:T(1,128)} %param.12) | copy-start | bytes 148
  59.5 30.3 %copy-start.2 = (s32[768]{0:T(1024)S(1)}, s32[768]{0:T(1024)}, u32[]{:S(2)}) copy-start(s32[768]{0:T(1024)} %param.15) | copy-start | bytes 9220
  65.2 8.5 %all-to-all-start.2 = ((f32[8,1,32]{2,1,0:T(1,128)}), f32[8,1,32]{2,1,0:T(1,128)S(1)}, u32[]{:S(2)}, u32[]{:S(2)}) async-start(f32[8,1,32]{2,1,0:T(1,128)} %broadcast_in_dim.49), calls=%async_computation.2 | async-start | bytes 8192 | tf_op jit(solution)/shard_map/all_to_all | solution.py:18
  74.4 11.1 %all-to-all-start.3 = ((f32[16,1,2]{2,1,0:T(1,128)}), f32[16,1,2]{2,1,0:T(1,128)S(1)}, u32[]{:S(2)}, u32[]{:S(2)}) async-start(f32[16,1,2]{2,1,0:T(1,128)} %bitcast.7), calls=%async_computation.3 | async-start | bytes 16384 | tf_op jit(solution)/shard_map/all_to_all | solution.py:121
  86.3 11.1 %all-to-all-start.4 = ((f32[16,1,48]{2,1,0:T(1,128)}), f32[16,1,48]{2,1,0:T(1,128)S(1)}, u32[]{:S(2)}, u32[]{:S(2)}) async-start(f32[16,1,48]{2,1,0:T(1,128)} %broadcast_in_dim.56), calls=%async_computation.4 | async-start | bytes 16384 | tf_op jit(solution)/shard_map/all_to_all | solution.py:18
  89.8 178.9 %reduce-scatter.2.cloned.1.call-start = ((), (), s32[]{:S(2)}) async-start(), calls=%async_computation.9 | async-start | bytes 14155776 | tf_op jit(solution)/shard_map/reduce_scatter | solution.py:152
  268.7 29.9 %all-to-all-start.6 = ((bf16[16,1024,48]{1,2,0:T(8,128)(2,1)}), bf16[16,1024,48]{1,2,0:T(8,128)(2,1)S(1)}, u32[]{:S(2)}, u32[]{:S(2)}) async-start(bf16[16,1024,48]{1,2,0:T(8,128)(2,1)} %bitcast.277), calls=%async_computation.7 | async-start | bytes 3145728 | tf_op jit(solution)/shard_map/all_to_all | solution.py:69
Sparse Core Ops, SparseCore 0:
  27.8 89.3 all-gather.9
  197.6 71.0 reduce-scatter.1
where the time goes:
time: 307 us; the launch traced here: 306 us
  waiting for transfers between devices  143 us (47%)
  blocking collectives  71.4 us (23%)
  matrix products  46 us (15%)
  starting transfers between devices  20.6 us (7%)
  between operations  14.4 us (5%)
  local copies, waits for them, and re-layouts  6.3 us (2%)
  other arithmetic  4.35 us (1%)
    reduce_scatter x1, waiting for transfers between devices, on_device(): lax.psum_scatter(lax.dot_general(head_weight, grad_logits, (((1,), (1,)),...  71.2 us
    all_gather x4, blocking collectives, all_in_one(): both, at, found = (lax.all_gather(jnp.concatenate(lines), axis), 0, {})  38.5 us
    all_to_all x3, waiting for transfers between devices, sent_to_all(): lax.all_to_all(jnp.broadcast_to(x[None], (size, *x.shape)), axis, 0, 0, t...  22.9 us
    all_to_all x1, waiting for transfers between devices, summed_on_arrival(): parts = lax.all_to_all(in_blocks(x, dim, size), axis, 0, 0, tiled=True)  22 us
    dot_general x1, matrix products, on_device(): lax.dot_general(head_weight, grad_logits, (((1,), (1,)), ((), ())), prefe...  21.9 us
    all_gather x1, waiting for transfers between devices, on_device(): lax.all_gather(feats, DP, axis=0, tiled=True)  19.7 us
    dot_general x1, matrix products, on_device(): jnp.dot(lax.all_gather(feats, DP, axis=0, tiled=True), head_weight, prefe...  18.7 us
    all_to_all x1, blocking collectives, sent_to_all(): lax.all_to_all(jnp.broadcast_to(x[None], (size, *x.shape)), axis, 0, 0, t...  18.4 us
  transfers between devices with their start and end apart: 7, of which 7 were waited for; matrix products, arithmetic and copies ran while one was open for 4% of the time, Pallas kernels for 0%

commit v1 on v0

--- a/solution.py
+++ b/solution.py
@@ -33,30 +33,12 @@
     return sent_to_all(x, axis).sum(axis=0)
 
 
-def all_in_one(x, axis):
-    leaves = jax.tree.leaves(x)
-    order = sorted(range(len(leaves)), key=lambda k: -leaves[k].size)
-    width = (1, *leaves[order[0]].shape)[-1]
-    lines = [
-        jnp.pad(leaves[k].reshape(-1), (0, -leaves[k].size % width)).reshape(-1, width)
-        for k in order
-    ]
-    both, at, found = (lax.all_gather(jnp.concatenate(lines), axis), 0, {})
-    for k, line in zip(order, lines):
-        slab = both[:, at : at + len(line)].reshape(len(both), -1)
-        found[k] = slab[:, : leaves[k].size].reshape(-1, *leaves[k].shape)
-        at += len(line)
-    numbers = iter(range(len(leaves)))
-    return jax.tree.map(lambda _: found[next(numbers)], x)
-
-
-def merged_by_axis(x, axes, combine):
-    for axis in axes:
-        pieces = all_in_one(x, axis)
-        x = jax.tree.map(lambda part: part[0], pieces)
-        for k in range(1, lax.axis_size(axis)):
-            x = combine(x, jax.tree.map(lambda part: part[k], pieces))
-    return x
+def merged_over(stats, axis):
+    both = sent_to_all(jnp.stack(stats), axis)
+    tops = both[:, 0]
+    top = jnp.max(tops, axis=0)
+    mass = jnp.sum(both[:, 1] * jnp.exp(tops - top[None, :]), axis=0)
+    return (top, mass, jnp.sum(both[:, 2], axis=0))
 
 
 def in_blocks(x, dim, size):
@@ -74,14 +56,6 @@
     return values * lax.rsqrt(jnp.mean(values * values, axis=-1, keepdims=True) + epsilon)
 
 
-def combine_rows(left_stats, right_stats):
-    joint_top = jnp.maximum(left_stats[0], right_stats[0])
-    joint_mass = left_stats[1] * jnp.exp(left_stats[0] - joint_top) + right_stats[1] * jnp.exp(
-        right_stats[0] - joint_top
-    )
-    return (joint_top, joint_mass, left_stats[2] + right_stats[2])
-
-
 def on_device(hidden, head_weight, critic_in, critic_out, rewards, turn_ids, owners, actions):
     ranks_dp = lax.axis_size(DP)
     ranks_vocab = lax.axis_size(VOCAB)
@@ -89,7 +63,6 @@
     turn_dev = rewards.shape[1]
     slot_count = max(2, 2 * turn_dev // ranks_dp)
     vocab_local = head_weight.shape[1]
-    feats = gather_directly(hidden, VOCAB, 1)
     position = jnp.arange(tok_dev, dtype=jnp.int32)
     turn_range = jnp.arange(turn_dev, dtype=jnp.int32)
     member = turn_ids[0][None, :] == turn_range[:, None]
@@ -128,27 +101,28 @@
     turn_value = jnp.sum(jnp.where(dispatch, values[None, :, :], 0.0), axis=(1, 2))
     advantage = rewards[0] - turn_value
     token_adv = jnp.sum(jnp.where(member, advantage[:, None], 0.0), axis=0)
-    token_adv_all = gather_directly(token_adv, DP, 0)
-    logits = jnp.dot(
-        lax.all_gather(feats, DP, axis=0, tiled=True),
-        head_weight,
+    spread = lax.all_gather(hidden, DP_VOCAB, axis=0, tiled=False)
+    spread = spread.reshape(ranks_dp, ranks_vocab, tok_dev, hidden.shape[1])
+    split_weight = head_weight.reshape(ranks_vocab, hidden.shape[1], vocab_local)
+    logits = lax.dot_general(
+        spread,
+        split_weight,
+        (((1, 3), (0, 1)), ((), ())),
         preferred_element_type=jnp.float32,
-    )
+    ).reshape(ranks_dp * tok_dev, vocab_local)
     first_col = (lax.axis_index(DP) * ranks_vocab + lax.axis_index(VOCAB)) * vocab_local
     local_action = actions - first_col
     hit = jnp.arange(vocab_local, dtype=jnp.int32)[None, :] == local_action[:, None]
     picked_part = jnp.sum(jnp.where(hit, logits, 0.0), axis=1)
     local_top = jnp.max(logits, axis=1)
     local_mass = jnp.sum(jnp.exp(logits - local_top[:, None]), axis=1)
-    row_top, row_mass, picked = merged_by_axis(
-        (local_top, local_mass, picked_part), DP_VOCAB, combine_rows
+    row_top, row_mass, picked = merged_over(
+        merged_over((local_top, local_mass, picked_part), VOCAB), DP
     )
     logprob_all = picked - row_top - jnp.log(row_mass)
     token_logprob = lax.dynamic_slice_in_dim(logprob_all, lax.axis_index(DP) * tok_dev, tok_dev, 0)
     probs = jnp.exp(logits - row_top[:, None]) / row_mass[:, None]
-    grad_logits = (loss_scale * token_adv_all[:, None] * (probs - hit.astype(jnp.float32))).astype(
-        jnp.bfloat16
-    )
+    grad_logits = (probs - hit.astype(jnp.float32)).astype(jnp.bfloat16)
     summed = lax.psum_scatter(
         lax.dot_general(
             head_weight, grad_logits, (((1,), (1,)), ((), ())), preferred_element_type=jnp.float32
@@ -157,7 +131,7 @@
         scatter_dimension=0,
         tiled=True,
     )
-    hidden_grad = summed_on_arrival(summed, DP, 1).T
+    hidden_grad = summed_on_arrival(summed, DP, 1).T * (loss_scale * token_adv[:, None])
     return (hidden_grad, token_logprob, advantage[None, :])
 
 

time: 307 us -> 287 us (0.935)
  waiting for transfers between devices: 143 us -> 91.4 us
  local copies, waits for them, and re-layouts: 6.3 us -> 42.9 us
  starting transfers between devices: 20.6 us -> 6.88 us
  matrix products: 46 us -> 57.8 us
    reduce_scatter x1, waiting for transfers between devices: 71.2 us -> 20.1 us  [on_device(): lax.psum_scatter(lax.dot_general(head_weight, grad_logits, (((1,), (1,)),...]
    all_gather x4 -> x0, blocking collectives: 38.5 us -> none  [all_in_one(): both, at, found = (lax.all_gather(jnp.concatenate(lines), axis), 0, {})]
    all_to_all x4 -> x0, waiting for transfers between devices: 30.5 us -> none  [the longest x3 22.9 us: sent_to_all(): lax.all_to_all(jnp.broadcast_to(x[None], (size, *x.shape)), axis, 0, 0, t...]
    all_gather x1, waiting for transfers between devices: 19.7 us -> 48.8 us  [on_device(): spread = lax.all_gather(hidden, DP_VOCAB, axis=0, tiled=False)]
    all_to_all x1 -> x4, blocking collectives: 18.4 us -> 46.7 us  [sent_to_all(): lax.all_to_all(jnp.broadcast_to(x[None], (size, *x.shape)), axis, 0, 0, t...]
    reshape x4 -> x2, local copies, waits for them, and re-layouts: 1 us -> 24.6 us  [the longest x1 13.7 us: on_device(): head_weight.reshape(ranks_vocab, hidden.shape[1], vocab_local)]
    unnamed x13 -> x14, local copies, waits for them, and re-layouts: 0.33 us -> 17 us
    all_to_all x4 -> x0, starting transfers between devices: 13.8 us -> none  [the longest x3 10.3 us: sent_to_all(): lax.all_to_all(jnp.broadcast_to(x[None], (size, *x.shape)), axis, 0, 0, t...]
  transfers between devices with their start and end apart: 7 -> 3, of which waited for: 7 -> 3; matrix products, arithmetic and copies ran while one was open for 4% -> 14% of each run, Pallas kernels for 0% -> 0%
where the time goes in v1:
time: 287 us; the launch traced here: 286 us
  waiting for transfers between devices  91.4 us (32%)
  blocking collectives  68.7 us (24%)
  matrix products  57.8 us (20%)
  local copies, waits for them, and re-layouts  42.9 us (15%)
  between operations  14.3 us (5%)
  starting transfers between devices  6.88 us (2%)
  other arithmetic  4.42 us (2%)
    all_gather x1, waiting for transfers between devices, on_device(): spread = lax.all_gather(hidden, DP_VOCAB, axis=0, tiled=False)  48.8 us
    all_to_all x4, blocking collectives, sent_to_all(): lax.all_to_all(jnp.broadcast_to(x[None], (size, *x.shape)), axis, 0, 0, t...  46.7 us
    dot_general x1, matrix products, on_device(): lax.dot_general(spread, split_weight, (((1, 3), (0, 1)), ((), ())), prefe...  30.5 us
    dot_general x1, matrix products, on_device(): lax.dot_general(head_weight, grad_logits, (((1,), (1,)), ((), ())), prefe...  21.8 us
    all_to_all x1, waiting for transfers between devices, summed_on_arrival(): parts = lax.all_to_all(in_blocks(x, dim, size), axis, 0, 0, tiled=True)  21.8 us
    reduce_scatter x1, waiting for transfers between devices, on_device(): lax.psum_scatter(lax.dot_general(head_weight, grad_logits, (((1,), (1,)),...  20.1 us
    unnamed x14, local copies, waits for them, and re-layouts  17 us
    reshape x1, local copies, waits for them, and re-layouts, on_device(): head_weight.reshape(ranks_vocab, hidden.shape[1], vocab_local)  13.7 us
  transfers between devices with their start and end apart: 3, of which 3 were waited for; matrix products, arithmetic and copies ran while one was open for 14% of the time, Pallas kernels for 0%

profile of v1, /device:TPU:0, one launch (start us, length us, event | category | flops | bytes accessed | tf_op | source)
XLA Modules:
  0.0 286.4 jit_solution(7687445112846692931)
XLA Ops:
  7.2 0.0 copy-start
  7.2 0.0 all-gather.3.cloned.1.call-start
  7.2 0.7 all-gather.3.cloned.1.call-update
  7.9 0.0 reduce-scatter.2.cloned.1.call-start
  8.0 0.0 copy-start.2
  8.0 16.1 %copy.57 = bf16[126,8,8,1024]{3,2,1,0:T(8,128)(2,1)} copy(bf16[126,8,8,1024]{3,1,2,0:T(8,128)(2,1)} %bitcast.95) | data formatting | bytes 33030144
  24.0 0.0 copy-done.2
  24.0 13.7 %slice_bitcast_fusion = bf16[8,1024,1002]{1,0,2:T(8,128)(2,1)} fusion(bf16[1008,8,1024]{2,1,0:T(8,128)(2,1)} %bitcast.94), kind=kLoop, calls=%fused_computation.2 | loop fusion | bytes 32833536 | tf_op jit(solution)/shard_map/reshape | solution.py:106
  37.7 48.8 %all-gather.3.cloned.1.call-done = bf16[6144,1024]{1,0:T(8,128)(2,1)} async-done(((bf16[48,1024]{1,0:T(8,128)(2,1)}), bf16[6144,1024]{1,0:T(8,128)(2,1)}) %all-gather.3.cloned.1.call-update) | async-done | bytes 12582928 | tf_op jit(solution)/shard_map/all_gather | solution.py:104
  86.6 10.9 %copy.37 = bf16[16,8,48,1024]{3,2,0,1:T(8,128)(2,1)} copy(bf16[16,8,48,1024]{3,2,1,0:T(8,128)(2,1)} %bitcast.96) | data formatting | bytes 25165824 | tf_op jit(solution)/shard_map/reshape | solution.py:105
  97.4 30.5 %bitcast_reduce_fusion = (f32[768]{0:T(1024)S(1)}, f32[768,1002,1]{0,1,2:T(8,128)S(1)}) fusion(bf16[768,8,1024]{2,0,1:T(8,128)(2,1)} %bitcast.97, bf16[8,1024,1002]{1,0,2:T(8,128)(2,1)} %slice_bitcast_fusion), kind=kOutput, calls=%fused_computation.11 | convolution fusion | flops 12608846848 | bytes 32080896 | tf_op jit(solution)/shard_map/dot_general | solution.py:107
  127.9 0.8 fusion.6
  128.8 9.6 %all_to_all.40 = f32[8,3,768]{2,1,0:T(4,128)S(1)} all-to-all(f32[8,3,768]{2,1,0:T(4,128)S(1)} %broadcast_in_dim.49), channel_id=1, replica_groups=mesh['dp_0'=4,'dp_1'=4,'vocab_0'=4,'vocab_1'=2] {'vocab_0','vocab_1'}, dimensions={0} | all-to-all | bytes 147456 | tf_op jit(solution)/shard_map/all_to_all | solution.py:18
  138.4 0.1 slice_reduce_fusion.2
  138.6 13.4 %all_to_all.41 = f32[16,3,768]{2,1,0:T(4,128)S(1)} all-to-all(f32[16,3,768]{2,1,0:T(4,128)S(1)} %broadcast_in_dim.50), channel_id=1, replica_groups=mesh['dp_0'=4,'dp_1'=4,'vocab_0'=4,'vocab_1'=2] {'dp_0','dp_1'}, dimensions={0} | all-to-all | bytes 294912 | tf_op jit(solution)/shard_map/all_to_all | solution.py:18
  152.0 0.1 slice_reduce_fusion
  152.2 21.8 %fusion.2 = bf16[8192,768]{0,1:T(8,128)(2,1)} fusion(bf16[8192,1002]{0,1:T(8,128)(2,1)} %param.9, f32[768,1002,1]{0,1,2:T(8,128)S(1)} %get-tuple-element.14, f32[768]{0:T(1024)S(1)} %fusion.26, f32[768]{0:T(1024)S(1)} %get-tuple-element.6, s32[768]{0:T(1024)S(1)} %broadcast_subtract_fusion), kind=kOutput, calls=%fused_computation.4 | convolution fusion | flops 12618986496 | bytes 32087040 | tf_op jit(solution)/shard_map/dot_general | solution.py:127
  174.0 0.0 copy-start.3
  174.0 0.0 copy-start.4
  174.0 0.0 reduce-scatter.2.cloned.1.call-update
  174.1 0.6 copy-done.3
  174.7 0.2 convert_reduce_fusion.1
  174.9 0.0 copy-done.4
  174.9 0.1 select_reduce_fusion.2
  175.1 0.0 copy-done.1
  175.1 0.3 convolution_convert_fusion.1
  175.4 11.1 %all_to_all.42 = bf16[16,2,1024]{2,1,0:T(2,128)(2,1)S(1)} all-to-all(bf16[16,2,1024]{2,1,0:T(2,128)(2,1)S(1)} %reshape.127), channel_id=1, replica_groups=mesh['dp_0'=4,'dp_1'=4,'vocab_0'=4,'vocab_1'=2] {'dp_0','dp_1'}, dimensions={0} | all-to-all | bytes 131072 | tf_op jit(solution)/shard_map/all_to_all | solution.py:86
  186.6 0.3 broadcast_in_dim.52
  186.8 15.9 %all_to_all.43 = bf16[8,16,2,1024]{3,2,1,0:T(2,128)(2,1)S(1)} all-to-all(bf16[8,16,2,1024]{3,2,1,0:T(2,128)(2,1)S(1)} %broadcast_in_dim.52), channel_id=1, replica_groups=mesh['dp_0'=4,'dp_1'=4,'vocab_0'=4,'vocab_1'=2] {'vocab_0','vocab_1'}, dimensions={0} | all-to-all | bytes 1048576 | tf_op jit(solution)/shard_map/all_to_all | solution.py:18
  202.7 0.6 fusion.16
  203.3 0.5 fusion.18
  203.9 0.3 copy.42
  204.2 0.3 copy.58
  204.5 0.0 copy-done
  204.5 5.2 %convolution_bitcast_fusion = f32[32]{0:T(128)S(1)} fusion(bf16[32,8192]{1,0:T(8,128)(2,1)S(1)} %bitcast.98, bf16[1,8192,512]{2,1,0:T(8,128)(2,1)} %param.10, bf16[1,512]{1,0:T(2,128)(2,1)S(1)} %copy-done), kind=kOutput, calls=%fused_computation.27 | convolution fusion | flops 268550144 | bytes 8914048 | tf_op jit(solution)/shard_map/dot_general | solution.py:92
  209.7 7.9 %all_to_all.44 = f32[8,1,32]{2,1,0:T(1,128)S(1)} all-to-all(f32[8,1,32]{2,1,0:T(1,128)S(1)} %broadcast_in_dim.53), channel_id=1, replica_groups=mesh['dp_0'=4,'dp_1'=4,'vocab_0'=4,'vocab_1'=2] {'vocab_0','vocab_1'}, dimensions={0} | all-to-all | bytes 2048 | tf_op jit(solution)/shard_map/all_to_all | solution.py:18
  217.6 0.1 all_to_all.31
  217.6 10.9 %all_to_all.45 = f32[16,1,2]{2,1,0:T(1,128)S(1)} all-to-all(f32[16,1,2]{2,1,0:T(1,128)S(1)} %bitcast.102), channel_id=1, replica_groups=mesh['dp_0'=4,'dp_1'=4,'vocab_0'=4,'vocab_1'=2] {'dp_0','dp_1'}, dimensions={0} | all-to-all | bytes 256 | tf_op jit(solution)/shard_map/all_to_all | solution.py:94
  228.5 20.1 %reduce-scatter.2.cloned.1.call-done = bf16[1024,768]{0,1:T(8,128)(2,1)} async-done(((bf16[8192,768]{0,1:T(8,128)(2,1)}), bf16[1024,768]{0,1:T(8,128)(2,1)}) %reduce-scatter.2.cloned.1.call-update) | async-done | bytes 1572880 | tf_op jit(solution)/shard_map/reduce_scatter | solution.py:126
  248.6 6.8 %all-to-all-start.2 = ((bf16[16,1024,48]{1,2,0:T(8,128)(2,1)}), bf16[16,1024,48]{1,2,0:T(8,128)(2,1)S(1)}, u32[]{:S(2)}, u32[]{:S(2)}) async-start(bf16[16,1024,48]{1,2,0:T(8,128)(2,1)} %bitcast.100), calls=%async_computation.3 | async-start | bytes 3145728 | tf_op jit(solution)/shard_map/all_to_all | solution.py:51
  255.4 0.1 select_reduce_fusion
  255.5 0.0 copy-done.5
  255.5 0.1 select_reduce_fusion.1
  255.6 0.5 bitcast_subtract_fusion.2
  256.1 0.6 dynamic_slice.3
  256.7 21.8 %all-to-all-done.2 = bf16[16,1024,48]{1,2,0:T(8,128)(2,1)S(1)} async-done(((bf16[16,1024,48]{1,2,0:T(8,128)(2,1)}), bf16[16,1024,48]{1,2,0:T(8,128)(2,1)S(1)}, u32[]{:S(2)}, u32[]{:S(2)}) %all-to-all-start.2) | async-done | bytes 1572896 | tf_op jit(solution)/shard_map/all_to_all | solution.py:51
  278.5 0.3 convert_reduce_fusion
  278.8 0.8 multiply_bitcast_fusion
  (26 shorter events, 0.3 us)
Async XLA Ops:
  7.2 197.3 %copy-start = (bf16[1,512]{1,0:T(2,128)(2,1)S(1)}, bf16[1,512]{1,0:T(2,128)(2,1)}, u32[]{:S(2)}) copy-start(bf16[1,512]{1,0:T(2,128)(2,1)} %param.11) | copy-start | bytes 3076
  7.2 79.4 %all-gather.3.cloned.1.call-start = ((), (), s32[]{:S(2)}) async-start(), calls=%async_computation.9 | async-start | bytes 12681216 | tf_op jit(solution)/shard_map/all_gather | solution.py:104
  7.9 240.7 %reduce-scatter.2.cloned.1.call-start = ((), (), s32[]{:S(2)}) async-start(), calls=%async_computation.8 | async-start | bytes 14155776 | tf_op jit(solution)/shard_map/reduce_scatter | solution.py:126
  8.0 16.1 %copy-start.2 = (s32[768]{0:T(1024)S(1)}, s32[768]{0:T(1024)}, u32[]{:S(2)}) copy-start(s32[768]{0:T(1024)} %param.15) | copy-start | bytes 9220
  174.0 0.7 copy-start.3
  174.0 0.9 copy-start.4
  174.0 1.0 copy-start.1
  209.7 45.9 %copy-start.5 = (f32[1,12]{1,0:T(1,128)S(1)}, f32[1,12]{1,0:T(1,128)}, u32[]{:S(2)}) copy-start(f32[1,12]{1,0:T(1,128)} %param.12) | copy-start | bytes 148
  248.6 29.9 %all-to-all-start.2 = ((bf16[16,1024,48]{1,2,0:T(8,128)(2,1)}), bf16[16,1024,48]{1,2,0:T(8,128)(2,1)S(1)}, u32[]{:S(2)}, u32[]{:S(2)}) async-start(bf16[16,1024,48]{1,2,0:T(8,128)(2,1)} %bitcast.100), calls=%async_computation.3 | async-start | bytes 3145728 | tf_op jit(solution)/shard_map/all_to_all | solution.py:51
Sparse Core Ops, SparseCore 0:
  11.0 75.5 all-gather.2
  174.2 74.3 reduce-scatter.1

commit v2 on v1

v2 whole, which is shorter than its diff:
```python
import functools

import jax
import jax.numpy as jnp
from jax import lax
from jax.experimental import pallas as pl
from jax.experimental.pallas import tpu as pltpu
from jax.sharding import Mesh
from jax.sharding import PartitionSpec as P


DP = ("dp_0", "dp_1")
VOCAB = ("vocab_0", "vocab_1")
DP_VOCAB = ("dp_0", "dp_1", "vocab_0", "vocab_1")
X, Y, Z, CORE = DP_VOCAB
SIDE = 4
LANES = 128
CHUNK = 256


epsilon = 1e-05
loss_scale = 32.0
f32 = jnp.float32
bf16 = jnp.bfloat16


def from_ahead(x, axis, k):
    return lax.ppermute(x, axis, [((i + k) % SIDE, i) for i in range(SIDE)])


def to_ahead(x, axis, k):
    return lax.ppermute(x, axis, [(i, (i + k) % SIDE) for i in range(SIDE)])


def to_partner(x):
    return lax.ppermute(x, CORE, [(0, 1), (1, 0)])


def over(x, axis):
    return lax.all_to_all(x, axis, 0, 0, tiled=True)


def to_lines(flat, lines):
    return jnp.pad(flat, (0, lines * LANES - flat.shape[0])).reshape(lines, LANES)


def gathered(hidden):
    ahead = [hidden] + [from_ahead(hidden, Z, k) for k in (1, 3, 2)]
    low = jnp.stack([ahead[0], ahead[1]])
    high = jnp.stack([ahead[3], ahead[2]])
    low_x = [low] + [from_ahead(low, X, k) for k in (1, 3, 2)]
    high_y = [high] + [from_ahead(high, Y, k) for k in (1, 3, 2)]
    low = jnp.stack([low_x[0], low_x[1], low_x[3], low_x[2]])
    high = jnp.stack([high_y[0], high_y[1], high_y[3], high_y[2]])
    a = {0: low} | {k: from_ahead(low, Y, k) for k in (1, 3, 2)}
    b = {0: high} | {k: from_ahead(high, X, k) for k in (1, 3, 2)}
    return [a[k] for k in range(SIDE)], [b[k] for k in range(SIDE)]


def logits_body(place, *refs):
    pieces = refs[:16]
    weight, critic, score, pick, local = refs[16:21]
    logits, stats, value = refs[21:24]
    rows, inner, squares = refs[24:]
    step = pl.program_id(0)
    tok = pieces[0].shape[2]
    for own in range(2):
        for grp in range(2):

            @pl.when(step // 2 == own * 2 + grp)
            def _(own=own, grp=grp):
                for k in range(SIDE):
                    piece = pieces[own * 8 + grp * 4 + k]
                    for j in range(SIDE):
                        at = (k * SIDE + j if grp == 0 else j * SIDE + k) * tok
                        rows[at : at + tok] = piece[j, 0]

    @pl.when(step == 0)
    def _():
        logits[...] = jnp.zeros(logits.shape, f32)
        inner[...] = jnp.zeros(inner.shape, f32)
        squares[...] = jnp.zeros(squares.shape, f32)

    for at in range(0, rows.shape[0], CHUNK):
        logits[:, at : at + CHUNK] += lax.dot_general(
            weight[...], rows[at : at + CHUNK], (((1,), (1,)), ((), ())), preferred_element_type=f32
        )
    ends = lax.dot_general(
        pick[...], rows[...], (((1,), (0,)), ((), ())), preferred_element_type=f32
    )
    inner[...] += jnp.dot(ends.astype(bf16), critic[0], preferred_element_type=f32)
    squares[...] += jnp.sum(ends * ends, axis=1, keepdims=True)

    @pl.when(step == 7)
    def _():
        full = logits[...]
        top = jnp.max(full, axis=0, keepdims=True)
        stats[0:1] = top
        stats[1:2] = jnp.sum(jnp.exp(full - top), axis=0, keepdims=True)
        ids = lax.broadcasted_iota(jnp.int32, full.shape, 0)
        stats[2:3] = jnp.sum(jnp.where(ids == local[0:1], full, 0.0), axis=0, keepdims=True)
        stats[3:8] = jnp.zeros((5, full.shape[1]), f32)
        mean = squares[:, :1] / (weight.shape[1] * 8)
        hid = inner[...] * lax.rsqrt(mean + epsilon)
        active = (hid / (1.0 + jnp.exp(-hid))).astype(bf16).astype(f32)
        out = jnp.sum(active * score[...].astype(f32), axis=1, keepdims=True)
        value[...] = jnp.broadcast_to(out, value.shape)


def feature_block(place, dz, other):
    return ((place[0] + dz) % SIDE) * 2 + (place[1] + other) % 2


def find_logits(place, pieces, weight, critic_in, critic_out, pick, local):
    vocab, _ = weight.shape
    tok, feat = pieces[0].shape[2:]
    hidden_units = critic_in.shape[2]
    slots, tokens = pick.shape

    def piece_spec(own, grp):
        first = own * 4 + grp * 2
        return pl.BlockSpec(
            (SIDE, 1, tok, feat), lambda s, p: (0, jnp.where(s > first, 1, 0), 0, 0)
        )

    whole = lambda shape: pl.BlockSpec(shape, lambda s, p: (0,) * len(shape))
    specs = [piece_spec(own, grp) for own in range(2) for grp in range(2) for _ in range(SIDE)]
    specs += [
        pl.BlockSpec((vocab, feat), lambda s, p: (0, feature_block(p, s % 4, s // 4))),
        pl.BlockSpec((1, feat, hidden_units), lambda s, p: (0, feature_block(p, s % 4, s // 4), 0)),
        whole((1, hidden_units)),
        whole((slots, tokens)),
        whole((8, tokens)),
    ]
    return pl.pallas_call(
        logits_body,
        grid_spec=pltpu.PrefetchScalarGridSpec(
            num_scalar_prefetch=1,
            grid=(8,),
            in_specs=specs,
            out_specs=[whole((vocab, tokens)), whole((8, tokens)), whole((slots, LANES))],
            scratch_shapes=[
                pltpu.VMEM((tokens, feat), bf16),
                pltpu.VMEM((slots, hidden_units), f32),
                pltpu.VMEM((slots, LANES), f32),
            ],
        ),
        out_shape=[
            jax.ShapeDtypeStruct((vocab, tokens), f32),
            jax.ShapeDtypeStruct((8, tokens), f32),
            jax.ShapeDtypeStruct((slots, LANES), f32),
        ],
        compiler_params=pltpu.CompilerParams(
            dimension_semantics=("arbitrary",), vmem_limit_bytes=56 * 2**20
        ),
        name="logits",
    )(place, *pieces, weight, critic_in, critic_out, pick, local)


def first_body(place, logits, stats, local, weight, grad, out, turned):
    vocab = logits.shape[0]

    @pl.when(pl.program_id(0) == 0)
    def _():
        ids = lax.broadcasted_iota(jnp.int32, logits.shape, 0)
        hit = jnp.where(ids == local[0:1], 1.0, 0.0)
        probs = jnp.exp(logits[...] - stats[0:1]) / stats[1:2]
        turned[vocab // 16 * 16 :] = jnp.zeros(
            (turned.shape[0] - vocab // 16 * 16, turned.shape[1]), bf16
        )
        turned[:vocab] = (probs - hit).astype(bf16)
        grad[...] = jnp.transpose(turned[...])[:, :vocab]

    out[0] = jnp.dot(grad[...], weight[...], preferred_element_type=f32).astype(bf16)


def next_body(place, grad, weight, out):
    out[0] = jnp.dot(grad[...], weight[...], preferred_element_type=f32).astype(bf16)


def last_body(grp, place, grad, weight, other, *outs):
    tok = outs[0].shape[2]
    both = jnp.dot(grad[...], weight[...], preferred_element_type=f32) + other[0].astype(f32)
    both = both.astype(bf16)
    for k in range(SIDE):
        for j in range(SIDE):
            at = (k * SIDE + j if grp == 0 else j * SIDE + k) * tok
            outs[k][j, 0] = both[at : at + tok]


def back(place, weight, grp, other_core, tok, feat, grad=None, softmax=None, received=None):
    vocab = weight.shape[0]
    tokens = SIDE * SIDE * tok
    whole = lambda shape: pl.BlockSpec(shape, lambda s, p: (0,) * len(shape))
    weight_spec = pl.BlockSpec(
        (vocab, feat), lambda s, p: (0, feature_block(p, s + 2 * grp, other_core))
    )
    tile = pl.BlockSpec((1, tokens, feat), lambda s, p: (s, 0, 0))
    tile_shape = jax.ShapeDtypeStruct((2, tokens, feat), bf16)
    scratch = []
    if softmax is not None:
        body = first_body
        args = (*softmax, weight)
        in_specs = [whole((vocab, tokens)), whole((8, tokens)), whole((8, tokens)), weight_spec]
        scratch = [pltpu.VMEM((-(-vocab // LANES) * LANES, tokens), bf16)]
        out_specs = [whole((tokens, vocab)), tile]
        out_shape = [jax.ShapeDtypeStruct((tokens, vocab), bf16), tile_shape]
    elif received is None:
        body = next_body
        args = (grad, weight)
        in_specs = [whole((tokens, vocab)), weight_spec]
        out_specs = [tile]
        out_shape = [tile_shape]
    else:
        body = functools.partial(last_body, grp)
        args = (grad, weight, received)
        in_specs = [whole((tokens, vocab)), weight_spec, tile]
        piece = pl.BlockSpec((SIDE, 1, tok, feat), lambda s, p: (0, s, 0, 0))
        out_specs = [piece] * SIDE
        out_shape = [jax.ShapeDtypeStruct((SIDE, 2, tok, feat), bf16)] * SIDE
    return pl.pallas_call(
        body,
        grid_spec=pltpu.PrefetchScalarGridSpec(
            num_scalar_prefetch=1,
            grid=(2,),
            in_specs=in_specs,
            out_specs=out_specs,
            scratch_shapes=scratch,
        ),
        out_shape=out_shape,
        compiler_params=pltpu.CompilerParams(
            dimension_semantics=("arbitrary",), vmem_limit_bytes=56 * 2**20
        ),
    )(place, *args)


def added(parts):
    total = parts[0].astype(f32)
    for part in parts[1:]:
        total = total + part.astype(f32)
    return total


def sent_and_added(pieces, axis):
    return added([pieces[0]] + [to_ahead(pieces[k], axis, k) for k in (1, 3, 2)])


def on_device(hidden, head_weight, critic_in, critic_out, rewards, turn_ids, owners, actions):
    tok_dev, feat = hidden.shape
    turn_dev = rewards.shape[1]
    ranks_dp = SIDE * SIDE
    tokens = ranks_dp * tok_dev
    slot_count = max(2, 2 * turn_dev // ranks_dp)
    slots = ranks_dp * slot_count
    vocab_local = head_weight.shape[1]
    weight = head_weight.T
    at_x, at_y, at_z, at_core = (lax.axis_index(axis) for axis in DP_VOCAB)
    place = jnp.stack([at_z, at_core]).astype(jnp.int32)

    def ahead_order(v):
        v = v.reshape(*v.shape[:-1], SIDE, SIDE, tok_dev)
        v = jnp.roll(jnp.roll(v, -at_x, axis=-3), -at_y, axis=-2)
        return jnp.swapaxes(v, -3, -2).reshape(*v.shape[:-3], tokens)

    def true_order(v):
        v = jnp.swapaxes(v.reshape(*v.shape[:-1], SIDE, SIDE, tok_dev), -3, -2)
        v = jnp.roll(jnp.roll(v, at_x, axis=-3), at_y, axis=-2)
        return v.reshape(*v.shape[:-3], tokens)

    low, high = gathered(hidden)
    pieces = low + high
    pieces = pieces + [to_partner(p) for p in pieces]

    position = jnp.arange(tok_dev, dtype=jnp.int32)
    turn_range = jnp.arange(turn_dev, dtype=jnp.int32)
    member = turn_ids[0][None, :] == turn_range[:, None]
    last_pos = jnp.max(jnp.where(member, position[None, :], -1), axis=1)
    owner_of = owners[:, 0]
    earlier = (owner_of[None, :] == owner_of[:, None]) & (turn_range[None, :] < turn_range[:, None])
    slot_of = jnp.sum(earlier.astype(jnp.int32), axis=1)
    dest_range = jnp.arange(ranks_dp, dtype=jnp.int32)
    slot_range = jnp.arange(slot_count, dtype=jnp.int32)
    dispatch = (owner_of[:, None, None] == dest_range[None, :, None]) & (
        slot_of[:, None, None] == slot_range[None, None, :]
    )
    spots = jnp.max(jnp.where(dispatch, last_pos[:, None, None], -1), axis=0).astype(f32)
    spots, _ = lax.optimization_barrier((spots, low[0]))
    wanted = over(spots, DP).reshape(slots).astype(jnp.int32)
    order = jnp.arange(tokens, dtype=jnp.int32)
    block_y = (order // (SIDE * tok_dev) + at_y) % SIDE
    block_x = (order // tok_dev % SIDE + at_x) % SIDE
    block = block_x * SIDE + block_y
    slot_range_all = jnp.arange(slots, dtype=jnp.int32)
    pick = (
        (slot_range_all[:, None] // slot_count == block[None, :])
        & (wanted[:, None] == (order % tok_dev)[None, :])
    ).astype(bf16)

    first_col = (lax.axis_index(DP) * (2 * SIDE) + at_z * 2 + at_core) * vocab_local
    local = jnp.broadcast_to(ahead_order(actions - first_col)[None], (8, tokens))

    logits, stats, value = find_logits(
        place, pieces, weight, critic_in, critic_out, pick, local
    )

    lines = (3 * tokens + slots + LANES - 1) // LANES
    message = to_lines(jnp.concatenate([stats[:3].reshape(-1), value[:, 0]]), lines)
    both = over(jnp.broadcast_to(message[None], (2 * SIDE, *message.shape)), VOCAB)
    both = both.reshape(2 * SIDE, -1)
    tops = both[:, :tokens]
    masses = both[:, tokens : 2 * tokens]
    top = jnp.max(tops, axis=0)
    mass = jnp.sum(masses * jnp.exp(tops - top[None]), axis=0)
    picked = jnp.sum(both[:, 2 * tokens : 3 * tokens], axis=0)
    values = jnp.sum(both[:, 3 * tokens : 3 * tokens + slots], axis=0)
    straight = true_order(jnp.stack([top, mass, picked]))
    shared = jnp.broadcast_to(straight[:2].reshape(1, -1), (ranks_dp, 2 * tokens))
    message = jnp.concatenate(
        [shared, straight[2].reshape(ranks_dp, tok_dev), values.reshape(ranks_dp, slot_count)],
        axis=1,
    )
    width = -(-message.shape[1] // LANES) * LANES
    message = jnp.pad(message, ((0, 0), (0, width - message.shape[1])))
    both = over(message.reshape(ranks_dp, -1, LANES), DP).reshape(ranks_dp, width)
    tops = both[:, :tokens]
    masses = both[:, tokens : 2 * tokens]
    top = jnp.max(tops, axis=0)
    mass = jnp.sum(masses * jnp.exp(tops - top[None]), axis=0)
    picked = jnp.sum(both[:, 2 * tokens : 2 * tokens + tok_dev], axis=0)
    values = both[:, 2 * tokens + tok_dev : 2 * tokens + tok_dev + slot_count]
    ordered = ahead_order(jnp.stack([top, mass]))
    token_logprob = picked - ordered[0, :tok_dev] - jnp.log(ordered[1, :tok_dev])
    turn_value = jnp.sum(jnp.where(dispatch, values[None], 0.0), axis=(1, 2))
    advantage = rewards[0] - turn_value
    token_adv = jnp.sum(jnp.where(member, advantage[:, None], 0.0), axis=0)

    softmax = (logits, jnp.pad(ordered, ((0, 6), (0, 0))), local)
    grad, out_low = back(place, weight, 0, 1, tok_dev, feat, softmax=softmax)
    in_low = to_partner(out_low)
    (out_high,) = back(place, weight, 1, 1, tok_dev, feat, grad=grad)
    in_high = to_partner(out_high)
    low = back(place, weight, 0, 0, tok_dev, feat, grad=grad, received=in_low)
    high = back(place, weight, 1, 0, tok_dev, feat, grad=grad, received=in_high)
    low = sent_and_added(low, Y).astype(bf16)
    high = sent_and_added(high, X).astype(bf16)
    low = sent_and_added([low[k] for k in range(SIDE)], X).astype(bf16)
    high = sent_and_added([high[k] for k in range(SIDE)], Y).astype(bf16)
    total = sent_and_added([low[0], low[1], high[0], high[1]], Z)
    hidden_grad = total * (loss_scale * token_adv[:, None])
    return (hidden_grad, token_logprob, advantage[None, :])


def solution(mesh):
    finer = Mesh(mesh.devices.reshape(4, 4, 4, 2), DP_VOCAB)

    return jax.shard_map(
        on_device,
        mesh=finer,
        in_specs=(
            P(DP, VOCAB),
            P(None, DP_VOCAB),
            P(DP, None, VOCAB),
            P(DP, VOCAB),
            P(DP, None),
            P(DP, None),
            P(DP, None),
            P(),
        ),
        out_specs=(P(DP, VOCAB), P(DP), P(DP, None)),
        check_vma=False,
    )
```

time: 287 us -> 292 us (1.017)
  Pallas kernels: 0 us -> 60 us
  starting transfers between devices: 6.88 us -> 65.2 us
  blocking collectives: 68.7 us -> 10.8 us
  matrix products: 57.8 us -> 0 us
  waiting for transfers between devices: 91.4 us -> 137 us
  local copies, waits for them, and re-layouts: 42.9 us -> 7.17 us
  between operations: 14.3 us -> 1.07 us
  other arithmetic: 4.42 us -> 8 us
    ppermute x0 -> x40, waiting for transfers between devices: none -> 124 us  [the longest x15 83.4 us: from_ahead(): return lax.ppermute(x, axis, [((i + k) % SIDE, i) for i in range(SIDE)])]
    pallas_call x0 -> x5, Pallas kernels: none -> 60 us  [the longest x4 32.5 us: back(): pl.pallas_call(body, grid_spec=pltpu.PrefetchScalarGridSpec(num_scalar_pr...]
    all_to_all x6 -> x1, blocking collectives: 68.7 us -> 10.8 us  [over(): return lax.all_to_all(x, axis, 0, 0, tiled=True)]
    dot_general x4 -> x0, matrix products: 57.8 us -> none  [the longest x1 30.5 us: on_device(): lax.dot_general(spread, split_weight, (((1, 3), (0, 1)), ((), ())), prefe...]
    ppermute x0 -> x40, starting transfers between devices: none -> 55.2 us  [the longest x15 29.6 us: from_ahead(): return lax.ppermute(x, axis, [((i + k) % SIDE, i) for i in range(SIDE)])]
    all_gather x1 -> x0, waiting for transfers between devices: 48.8 us -> none  [on_device(): spread = lax.all_gather(hidden, DP_VOCAB, axis=0, tiled=False)]
    reshape x3 -> x5, local copies, waits for them, and re-layouts: 24.6 us -> 0.28 us  [the longest x1 0.08 us: ahead_order(): return jnp.swapaxes(v, -3, -2).reshape(*v.shape[:-3], tokens)]
    reduce_scatter x1 -> x0, waiting for transfers between devices: 20.1 us -> none  [on_device(): lax.psum_scatter(lax.dot_general(head_weight, grad_logits, (((1,), (1,)),...]
  transfers between devices with their start and end apart: 3 -> 42, of which waited for: 3 -> 20; matrix products, arithmetic and copies ran while one was open for 14% -> 3% of each run, Pallas kernels for 0% -> 6%
where the time goes in v2:
time: 292 us; the launch traced here: 289 us
  waiting for transfers between devices  137 us (47%)
  starting transfers between devices  65.2 us (22%)
  Pallas kernels  60 us (21%)
  blocking collectives  10.8 us (4%)
  other arithmetic  8 us (3%)
  local copies, waits for them, and re-layouts  7.17 us (2%)
    ppermute x15, waiting for transfers between devices, from_ahead(): return lax.ppermute(x, axis, [((i + k) % SIDE, i) for i in range(SIDE)])  83.4 us
    ppermute x15, waiting for transfers between devices, to_ahead(): return lax.ppermute(x, axis, [(i, (i + k) % SIDE) for i in range(SIDE)])  35.1 us
    pallas_call x4, Pallas kernels, back(): pl.pallas_call(body, grid_spec=pltpu.PrefetchScalarGridSpec(num_scalar_pr...  32.5 us
    ppermute x15, starting transfers between devices, from_ahead(): return lax.ppermute(x, axis, [((i + k) % SIDE, i) for i in range(SIDE)])  29.6 us
    pallas_call x1, Pallas kernels, find_logits(): pl.pallas_call(logits_body, grid_spec=pltpu.PrefetchScalarGridSpec(num_sc...  27.4 us
    ppermute x15, starting transfers between devices, to_ahead(): return lax.ppermute(x, axis, [(i, (i + k) % SIDE) for i in range(SIDE)])  23.8 us
    all_to_all x2, waiting for transfers between devices, over(): return lax.all_to_all(x, axis, 0, 0, tiled=True)  13.2 us
    all_to_all x1, blocking collectives, over(): return lax.all_to_all(x, axis, 0, 0, tiled=True)  10.8 us
  transfers between devices with their start and end apart: 42, of which 20 were waited for; matrix products, arithmetic and copies ran while one was open for 3% of the time, Pallas kernels for 6%

profile of v2, /device:TPU:0, one launch (start us, length us, event | category | flops | bytes accessed | tf_op | source)
XLA Modules:
  0.0 289.2 jit_solution(10071118055212679704)
XLA Ops:
  0.6 4.2 %collective-permute-start = (bf16[48,1024]{1,0:T(8,128)(2,1)}, bf16[48,1024]{1,0:T(8,128)(2,1)S(1)}, u32[]{:S(2)}, u32[]{:S(2)}) collective-permute-start(bf16[48,1024]{1,0:T(8,128)(2,1)} %param.8), channel_id=1, source_target_pairs={{2,0},{4,2},{6,4},{0,6},{3,1},{5,3},{7,5},{1,7},{10,8},{12,10},{14... | collective-permute-start | bytes 294920 | tf_op jit(solution)/shard_map/ppermute | solution.py:28
  4.9 2.5 collective-permute-done
  8.3 3.1 %collective-permute-start.2 = (bf16[2,48,1024]{2,1,0:T(8,128)(2,1)S(1)}, bf16[2,48,1024]{2,1,0:T(8,128)(2,1)S(1)}, u32[]{:S(2)}, u32[]{:S(2)}) collective-permute-start(bf16[2,48,1024]{2,1,0:T(8,128)(2,1)S(1)} %get-tuple-element.44), channel_id=1, source_target_pairs={{64,0},{96,32},{0,64},{32,96},{65,1},{97,33},{1,65},{33,97},{66,2}... | collective-permute-start | bytes 589832 | tf_op jit(solution)/shard_map/ppermute | solution.py:28
  11.4 1.1 collective-permute-start.1
  13.7 4.7 %collective-permute-start.7 = (bf16[48,1024]{1,0:T(8,128)(2,1)}, bf16[48,1024]{1,0:T(8,128)(2,1)S(1)}, u32[]{:S(2)}, u32[]{:S(2)}) collective-permute-start(bf16[48,1024]{1,0:T(8,128)(2,1)} %param.8), channel_id=1, source_target_pairs={{4,0},{6,2},{0,4},{2,6},{5,1},{7,3},{1,5},{3,7},{12,8},{14,10},{8,... | collective-permute-start | bytes 294920 | tf_op jit(solution)/shard_map/ppermute | solution.py:28
  18.4 1.6 collective-permute-done.1
  20.6 1.6 collective-permute-start.6
  22.3 2.9 %collective-permute-start.5 = (bf16[4,2,48,1024]{3,2,1,0:T(8,128)(2,1)S(1)}, bf16[4,2,48,1024]{3,2,1,0:T(8,128)(2,1)}, u32[]{:S(2)}, u32[]{:S(2)}) collective-permute-start(bf16[4,2,48,1024]{3,2,1,0:T(8,128)(2,1)S(1)} %pad_maximum_fusion.refs_0_), channel_id=1, source_target_pairs={{16,0},{24,8},{0,16},{8,24},{17,1},{25,9},{1,17},{9,25},{18,2},{26... | collective-permute-start | bytes 2359304 | tf_op jit(solution)/shard_map/ppermute | solution.py:28
  25.2 1.3 collective-permute-start.4
  27.0 37.1 %collective-permute-done.10 = bf16[2,48,1024]{2,1,0:T(8,128)(2,1)S(1)} collective-permute-done((bf16[2,48,1024]{2,1,0:T(8,128)(2,1)S(1)}, bf16[2,48,1024]{2,1,0:T(8,128)(2,1)S(1)}, u32[]{:S(2)}, u32[]{:S(2)}) %collective-permute-start.10) | collective-permute-done | bytes 196640 | tf_op jit(solution)/shard_map/ppermute | solution.py:28
  64.1 2.1 collective-permute-start.9
  66.4 4.1 %collective-permute-done.9 = bf16[2,48,1024]{2,1,0:T(8,128)(2,1)S(1)} collective-permute-done((bf16[2,48,1024]{2,1,0:T(8,128)(2,1)S(1)}, bf16[2,48,1024]{2,1,0:T(8,128)(2,1)S(1)}, u32[]{:S(2)}, u32[]{:S(2)}) %collective-permute-start.9) | collective-permute-done | bytes 196640 | tf_op jit(solution)/shard_map/ppermute | solution.py:28
  70.5 1.7 collective-permute-start.11
  72.3 5.1 %collective-permute-done.11 = bf16[2,48,1024]{2,1,0:T(8,128)(2,1)S(1)} collective-permute-done((bf16[2,48,1024]{2,1,0:T(8,128)(2,1)S(1)}, bf16[2,48,1024]{2,1,0:T(8,128)(2,1)S(1)}, u32[]{:S(2)}, u32[]{:S(2)}) %collective-permute-start.11) | collective-permute-done | bytes 196640 | tf_op jit(solution)/shard_map/ppermute | solution.py:28
  77.4 1.0 pad_maximum_fusion.1.refs_4_
  78.5 1.1 collective-permute-start.14
  79.6 2.7 collective-permute-start.13
  82.3 1.4 collective-permute-start.12
  84.8 15.1 %collective-permute-done.14.refs_7_ = bf16[4,2,48,1024]{3,2,1,0:T(8,128)(2,1)} collective-permute-done((bf16[4,2,48,1024]{3,2,1,0:T(8,128)(2,1)S(1)}, bf16[4,2,48,1024]{3,2,1,0:T(8,128)(2,1)}, u32[]{:S(2)}, u32[]{:S(2)}) %collective-permute-start.14) | collective-permute-done | bytes 786464 | tf_op jit(solution)/shard_map/ppermute | solution.py:28
  99.9 17.2 %collective-permute-done.13.refs_6_ = bf16[4,2,48,1024]{3,2,1,0:T(8,128)(2,1)} collective-permute-done((bf16[4,2,48,1024]{3,2,1,0:T(8,128)(2,1)S(1)}, bf16[4,2,48,1024]{3,2,1,0:T(8,128)(2,1)}, u32[]{:S(2)}, u32[]{:S(2)}) %collective-permute-start.13) | collective-permute-done | bytes 786464 | tf_op jit(solution)/shard_map/ppermute | solution.py:28
  119.2 5.3 %all-to-all-start = ((f32[16,1,2]{2,1,0:T(1,128)}), f32[16,1,2]{2,1,0:T(1,128)S(1)}, u32[]{:S(2)}, u32[]{:S(2)}) async-start(f32[16,1,2]{2,1,0:T(1,128)} %copy.24), calls=%async_computation | async-start | bytes 16384 | tf_op jit(solution)/shard_map/all_to_all | solution.py:40
  124.6 7.4 %all-to-all-done = f32[16,1,2]{2,1,0:T(1,128)S(1)} async-done(((f32[16,1,2]{2,1,0:T(1,128)}), f32[16,1,2]{2,1,0:T(1,128)S(1)}, u32[]{:S(2)}, u32[]{:S(2)}) %all-to-all-start) | async-done | bytes 160 | tf_op jit(solution)/shard_map/all_to_all | solution.py:40
  133.5 27.4 %logits.1 = (f32[1002,768]{1,0:T(8,128)}, f32[8,768]{1,0:T(8,128)}, f32[32,128]{1,0:T(8,128)}) custom-call(s32[2]{0:T(128)} %pad_add_fusion.place, bf16[4,2,48,1024]{3,2,1,0:T(8,128)(2,1)} %copy-done.1, bf16[4,2,48,1024]{3,2,1,0:T(8,128)(2,1)} %collective-permute-done.4.refs_1_, bf16[4,2,48,1024]{3,2,1,0:T(8,128)(2,1)} %collective-permute-done.5.refs_2_, ...), custom_call_target="tpu_custom_call" | custom-call | tf_op jit(solution)/shard_map/logits/pallas_call | solution.py:135
  163.2 4.6 %all-to-all-start.1 = ((f32[8,19,128]{2,1,0:T(8,128)}), f32[8,19,128]{2,1,0:T(8,128)S(1)}, u32[]{:S(2)}, u32[]{:S(2)}) async-start(f32[8,19,128]{2,1,0:T(8,128)} %broadcast_in_dim.94), calls=%async_computation.1 | async-start | bytes 196608 | tf_op jit(solution)/shard_map/all_to_all | solution.py:40
  167.8 5.8 %all-to-all-done.1 = f32[8,19,128]{2,1,0:T(8,128)S(1)} async-done(((f32[8,19,128]{2,1,0:T(8,128)}), f32[8,19,128]{2,1,0:T(8,128)S(1)}, u32[]{:S(2)}, u32[]{:S(2)}) %all-to-all-start.1) | async-done | bytes 77856 | tf_op jit(solution)/shard_map/all_to_all | solution.py:40
  174.4 10.8 %all_to_all.19 = f32[16,13,128]{2,1,0:T(8,128)S(1)} all-to-all(f32[16,13,128]{2,1,0:T(8,128)S(1)} %reshape.235), channel_id=1, replica_groups=mesh['dp_0'=4,'dp_1'=4,'vocab_0'=4,'vocab_1'=2] {'dp_0','dp_1'}, dimensions={0} | all-to-all | bytes 212992 | tf_op jit(solution)/shard_map/all_to_all | solution.py:40
  186.3 8.9 %shard_map.106 = (bf16[768,1002]{1,0:T(8,128)(2,1)}, bf16[2,768,1024]{2,1,0:T(8,128)(2,1)}) custom-call(s32[2]{0:T(128)} %pad_add_fusion.place, f32[1002,768]{1,0:T(8,128)} %get-tuple-element.18.logits, f32[8,768]{1,0:T(8,128)} %pad.14.stats, s32[8,768]{1,0:T(8,128)} %broadcast_in_dim.92.refs_20_.local, bf16[1002,8192]{1,0:T(8,128)(2,1)} %bitcast.85), custom_call_target="tpu_custom_call" | custom-call | tf_op jit(solution)/shard_map/pallas_call | solution.py:221
  195.2 7.6 %shard_map.108 = bf16[2,768,1024]{2,1,0:T(8,128)(2,1)} custom-call(s32[2]{0:T(128)} %pad_add_fusion.place, bf16[768,1002]{1,0:T(8,128)(2,1)} %get-tuple-element.21.grad, bf16[1002,8192]{1,0:T(8,128)(2,1)} %bitcast.86), custom_call_target="tpu_custom_call" | custom-call | tf_op jit(solution)/shard_map/pallas_call | solution.py:221
  203.4 5.3 %collective-permute-done.31.other = bf16[2,768,1024]{2,1,0:T(8,128)(2,1)} collective-permute-done((bf16[2,768,1024]{2,1,0:T(8,128)(2,1)}, bf16[2,768,1024]{2,1,0:T(8,128)(2,1)}, u32[]{:S(2)}, u32[]{:S(2)}) %collective-permute-start.31) | collective-permute-done | bytes 3145760 | tf_op jit(solution)/shard_map/ppermute | solution.py:36
  208.8 8.0 %shard_map.109 = (bf16[4,2,48,1024]{3,2,1,0:T(8,128)(2,1)}, bf16[4,2,48,1024]{3,2,1,0:T(8,128)(2,1)}, bf16[4,2,48,1024]{3,2,1,0:T(8,128)(2,1)}, bf16[4,2,48,1024]{3,2,1,0:T(8,128)(2,1)}) custom-call(s32[2]{0:T(128)} %pad_add_fusion.place, bf16[768,1002]{1,0:T(8,128)(2,1)} %get-tuple-element.21.grad, bf16[1002,8192]{1,0:T(8,128)(2,1)} %bitcast.87, ...), custom_call_target="tpu_custom_call" | custom-call | tf_op jit(solution)/shard_map/pallas_call | solution.py:221
  217.6 2.8 collective-permute-start.33
  221.0 1.6 copy-done
  222.7 8.0 %shard_map.107 = (bf16[4,2,48,1024]{3,2,1,0:T(8,128)(2,1)}, bf16[4,2,48,1024]{3,2,1,0:T(8,128)(2,1)}, bf16[4,2,48,1024]{3,2,1,0:T(8,128)(2,1)}, bf16[4,2,48,1024]{3,2,1,0:T(8,128)(2,1)}) custom-call(s32[2]{0:T(128)} %pad_add_fusion.place, bf16[768,1002]{1,0:T(8,128)(2,1)} %get-tuple-element.21.grad, bf16[1002,8192]{1,0:T(8,128)(2,1)} %bitcast.88, ...), custom_call_target="tpu_custom_call" | custom-call | tf_op jit(solution)/shard_map/pallas_call | solution.py:221
  231.2 2.8 collective-permute-start.25
  233.9 20.7 %collective-permute-done.32 = bf16[4,2,48,1024]{3,2,1,0:T(8,128)(2,1)S(1)} collective-permute-done((bf16[4,2,48,1024]{3,2,1,0:T(8,128)(2,1)}, bf16[4,2,48,1024]{3,2,1,0:T(8,128)(2,1)S(1)}, u32[]{:S(2)}, u32[]{:S(2)}) %collective-permute-start.32) | collective-permute-done | bytes 786464 | tf_op jit(solution)/shard_map/ppermute | solution.py:32
  254.7 1.5 collective-permute-start.26
  258.1 2.5 collective-permute-start.37
  260.6 1.6 collective-permute-start.36
  262.1 4.2 %collective-permute-done.25 = bf16[4,2,48,1024]{3,2,1,0:T(8,128)(2,1)S(1)} collective-permute-done((bf16[4,2,48,1024]{3,2,1,0:T(8,128)(2,1)}, bf16[4,2,48,1024]{3,2,1,0:T(8,128)(2,1)S(1)}, u32[]{:S(2)}, u32[]{:S(2)}) %collective-permute-start.25) | collective-permute-done | bytes 786464 | tf_op jit(solution)/shard_map/ppermute | solution.py:32
  266.3 5.4 %collective-permute-done.26 = bf16[4,2,48,1024]{3,2,1,0:T(8,128)(2,1)S(1)} collective-permute-done((bf16[4,2,48,1024]{3,2,1,0:T(8,128)(2,1)}, bf16[4,2,48,1024]{3,2,1,0:T(8,128)(2,1)S(1)}, u32[]{:S(2)}, u32[]{:S(2)}) %collective-permute-start.26) | collective-permute-done | bytes 786464 | tf_op jit(solution)/shard_map/ppermute | solution.py:32
  272.4 2.1 collective-permute-start.27
  274.5 2.2 collective-permute-start.29
  276.7 2.5 collective-permute-start.28
  279.4 1.2 collective-permute-start.38
  280.6 1.5 collective-permute-start.39
  282.6 1.4 collective-permute-start.30
  284.1 2.7 collective-permute-done.39
  286.8 1.7 collective-permute-done.30
  (143 shorter events, 18.6 us)
Async XLA Ops:
  0.6 65.6 %copy-start.9 = (s32[12,1]{0,1:T(1,128)S(1)}, s32[12,1]{0,1:T(1,128)}, u32[]{:S(2)}) copy-start(s32[12,1]{0,1:T(1,128)} %param.14) | copy-start | bytes 148
  0.6 6.7 %collective-permute-start = (bf16[48,1024]{1,0:T(8,128)(2,1)}, bf16[48,1024]{1,0:T(8,128)(2,1)S(1)}, u32[]{:S(2)}, u32[]{:S(2)}) collective-permute-start(bf16[48,1024]{1,0:T(8,128)(2,1)} %param.8), channel_id=1, source_target_pairs={{2,0},{4,2},{6,4},{0,6},{3,1},{5,3},{7,5},{1,7},{10,8},{12,10},{14... | collective-permute-start | bytes 294920 | tf_op jit(solution)/shard_map/ppermute | solution.py:28
  8.3 10.1 %collective-permute-start.2 = (bf16[2,48,1024]{2,1,0:T(8,128)(2,1)S(1)}, bf16[2,48,1024]{2,1,0:T(8,128)(2,1)S(1)}, u32[]{:S(2)}, u32[]{:S(2)}) collective-permute-start(bf16[2,48,1024]{2,1,0:T(8,128)(2,1)S(1)} %get-tuple-element.44), channel_id=1, source_target_pairs={{64,0},{96,32},{0,64},{32,96},{65,1},{97,33},{1,65},{33,97},{66,2}... | collective-permute-start | bytes 589832 | tf_op jit(solution)/shard_map/ppermute | solution.py:28
  11.4 8.6 %collective-permute-start.1 = (bf16[2,48,1024]{2,1,0:T(8,128)(2,1)S(1)}, bf16[2,48,1024]{2,1,0:T(8,128)(2,1)S(1)}, u32[]{:S(2)}, u32[]{:S(2)}) collective-permute-start(bf16[2,48,1024]{2,1,0:T(8,128)(2,1)S(1)} %get-tuple-element.44), channel_id=1, source_target_pairs={{32,0},{64,32},{96,64},{0,96},{33,1},{65,33},{97,65},{1,97},{34,2}... | collective-permute-start | bytes 589832 | tf_op jit(solution)/shard_map/ppermute | solution.py:28
  12.6 7.9 %collective-permute-start.3 = (bf16[2,48,1024]{2,1,0:T(8,128)(2,1)S(1)}, bf16[2,48,1024]{2,1,0:T(8,128)(2,1)S(1)}, u32[]{:S(2)}, u32[]{:S(2)}) collective-permute-start(bf16[2,48,1024]{2,1,0:T(8,128)(2,1)S(1)} %get-tuple-element.44), channel_id=1, source_target_pairs={{96,0},{0,32},{32,64},{64,96},{97,1},{1,33},{33,65},{65,97},{98,2}... | collective-permute-start | bytes 589832 | tf_op jit(solution)/shard_map/ppermute | solution.py:28
  13.4 11.8 %collective-permute-start.8 = (bf16[48,1024]{1,0:T(8,128)(2,1)}, bf16[48,1024]{1,0:T(8,128)(2,1)S(1)}, u32[]{:S(2)}, u32[]{:S(2)}) collective-permute-start(bf16[48,1024]{1,0:T(8,128)(2,1)} %param.8), channel_id=1, source_target_pairs={{6,0},{0,2},{2,4},{4,6},{7,1},{1,3},{3,5},{5,7},{14,8},{8,10},{10,... | collective-permute-start | bytes 294920 | tf_op jit(solution)/shard_map/ppermute | solution.py:28
  13.7 12.8 %collective-permute-start.7 = (bf16[48,1024]{1,0:T(8,128)(2,1)}, bf16[48,1024]{1,0:T(8,128)(2,1)S(1)}, u32[]{:S(2)}, u32[]{:S(2)}) collective-permute-start(bf16[48,1024]{1,0:T(8,128)(2,1)} %param.8), channel_id=1, source_target_pairs={{4,0},{6,2},{0,4},{2,6},{5,1},{7,3},{1,5},{3,7},{12,8},{14,10},{8,... | collective-permute-start | bytes 294920 | tf_op jit(solution)/shard_map/ppermute | solution.py:28
  20.4 63.3 %copy-start.10 = (s32[1,48]{1,0:T(1,128)S(1)}, s32[1,48]{1,0:T(1,128)}, u32[]{:S(2)}) copy-start(s32[1,48]{1,0:T(1,128)} %param.13) | copy-start | bytes 580
  20.4 63.6 %copy-start.8 = (s32[768]{0:T(1024)S(1)}, s32[768]{0:T(1024)}, u32[]{:S(2)}) copy-start(s32[768]{0:T(1024)} %param.15) | copy-start | bytes 9220
  20.5 113.0 %copy-start.1 = (bf16[4,2,48,1024]{3,2,1,0:T(8,128)(2,1)}, bf16[4,2,48,1024]{3,2,1,0:T(8,128)(2,1)S(1)}, u32[]{:S(2)}) copy-start(bf16[4,2,48,1024]{3,2,1,0:T(8,128)(2,1)S(1)} %pad_maximum_fusion.refs_0_) | copy-start | bytes 2359300
  20.6 58.0 %collective-permute-start.15 = (bf16[4,2,48,1024]{3,2,1,0:T(8,128)(2,1)S(1)}, bf16[4,2,48,1024]{3,2,1,0:T(8,128)(2,1)S(1)}, u32[]{:S(2)}, u32[]{:S(2)}) collective-permute-start(bf16[4,2,48,1024]{3,2,1,0:T(8,128)(2,1)S(1)} %pad_maximum_fusion.refs_0_), channel_id=1, source_target_pairs={{0,1},{1,0},{2,3},{3,2},{4,5},{5,4},{6,7},{7,6},{8,9},{9,8},{10,11... | collective-permute-start | bytes 2359304 | tf_op jit(solution)/shard_map/ppermute | solution.py:36
  20.6 58.9 %collective-permute-start.6 = (bf16[4,2,48,1024]{3,2,1,0:T(8,128)(2,1)S(1)}, bf16[4,2,48,1024]{3,2,1,0:T(8,128)(2,1)S(1)}, u32[]{:S(2)}, u32[]{:S(2)}) collective-permute-start(bf16[4,2,48,1024]{3,2,1,0:T(8,128)(2,1)S(1)} %pad_maximum_fusion.refs_0_), channel_id=1, source_target_pairs={{24,0},{0,8},{8,16},{16,24},{25,1},{1,9},{9,17},{17,25},{26,2},{2,... | collective-permute-start | bytes 2359304 | tf_op jit(solution)/shard_map/ppermute | solution.py:28
  22.3 60.0 %collective-permute-start.5 = (bf16[4,2,48,1024]{3,2,1,0:T(8,128)(2,1)S(1)}, bf16[4,2,48,1024]{3,2,1,0:T(8,128)(2,1)}, u32[]{:S(2)}, u32[]{:S(2)}) collective-permute-start(bf16[4,2,48,1024]{3,2,1,0:T(8,128)(2,1)S(1)} %pad_maximum_fusion.refs_0_), channel_id=1, source_target_pairs={{16,0},{24,8},{0,16},{8,24},{17,1},{25,9},{1,17},{9,25},{18,2},{26... | collective-permute-start | bytes 2359304 | tf_op jit(solution)/shard_map/ppermute | solution.py:28
  25.2 58.5 %collective-permute-start.4 = (bf16[4,2,48,1024]{3,2,1,0:T(8,128)(2,1)S(1)}, bf16[4,2,48,1024]{3,2,1,0:T(8,128)(2,1)}, u32[]{:S(2)}, u32[]{:S(2)}) collective-permute-start(bf16[4,2,48,1024]{3,2,1,0:T(8,128)(2,1)S(1)} %pad_maximum_fusion.refs_0_), channel_id=1, source_target_pairs={{8,0},{16,8},{24,16},{0,24},{9,1},{17,9},{25,17},{1,25},{10,2},{18... | collective-permute-start | bytes 2359304 | tf_op jit(solution)/shard_map/ppermute | solution.py:28
  26.6 37.5 %collective-permute-start.10 = (bf16[2,48,1024]{2,1,0:T(8,128)(2,1)S(1)}, bf16[2,48,1024]{2,1,0:T(8,128)(2,1)S(1)}, u32[]{:S(2)}, u32[]{:S(2)}) collective-permute-start(bf16[2,48,1024]{2,1,0:T(8,128)(2,1)S(1)} %get-tuple-element.42), channel_id=1, source_target_pairs={{16,0},{24,8},{0,16},{8,24},{17,1},{25,9},{1,17},{9,25},{18,2},{26... | collective-permute-start | bytes 589832 | tf_op jit(solution)/shard_map/ppermute | solution.py:28
  64.1 6.4 %collective-permute-start.9 = (bf16[2,48,1024]{2,1,0:T(8,128)(2,1)S(1)}, bf16[2,48,1024]{2,1,0:T(8,128)(2,1)S(1)}, u32[]{:S(2)}, u32[]{:S(2)}) collective-permute-start(bf16[2,48,1024]{2,1,0:T(8,128)(2,1)S(1)} %get-tuple-element.42), channel_id=1, source_target_pairs={{8,0},{16,8},{24,16},{0,24},{9,1},{17,9},{25,17},{1,25},{10,2},{18... | collective-permute-start | bytes 589832 | tf_op jit(solution)/shard_map/ppermute | solution.py:28
  70.5 6.9 %collective-permute-start.11 = (bf16[2,48,1024]{2,1,0:T(8,128)(2,1)S(1)}, bf16[2,48,1024]{2,1,0:T(8,128)(2,1)S(1)}, u32[]{:S(2)}, u32[]{:S(2)}) collective-permute-start(bf16[2,48,1024]{2,1,0:T(8,128)(2,1)S(1)} %get-tuple-element.42), channel_id=1, source_target_pairs={{24,0},{0,8},{8,16},{16,24},{25,1},{1,9},{9,17},{17,25},{26,2},{2,... | collective-permute-start | bytes 589832 | tf_op jit(solution)/shard_map/ppermute | solution.py:28
  78.4 55.1 %copy-start.2 = (bf16[4,2,48,1024]{3,2,1,0:T(8,128)(2,1)}, bf16[4,2,48,1024]{3,2,1,0:T(8,128)(2,1)S(1)}, u32[]{:S(2)}) copy-start(bf16[4,2,48,1024]{3,2,1,0:T(8,128)(2,1)S(1)} %pad_maximum_fusion.1.refs_4_) | copy-start | bytes 2359300
  78.4 5.8 %collective-permute-start.19 = (bf16[4,2,48,1024]{3,2,1,0:T(8,128)(2,1)S(1)}, bf16[4,2,48,1024]{3,2,1,0:T(8,128)(2,1)}, u32[]{:S(2)}, u32[]{:S(2)}) collective-permute-start(bf16[4,2,48,1024]{3,2,1,0:T(8,128)(2,1)S(1)} %pad_maximum_fusion.1.refs_4_), channel_id=1, source_target_pairs={{0,1},{1,0},{2,3},{3,2},{4,5},{5,4},{6,7},{7,6},{8,9},{9,8},{10,11... | collective-permute-start | bytes 2359304 | tf_op jit(solution)/shard_map/ppermute | solution.py:36
  78.5 55.0 %copy-start.5 = (bf16[4,2,48,1024]{3,2,1,0:T(8,128)(2,1)}, bf16[4,2,48,1024]{3,2,1,0:T(8,128)(2,1)S(1)}, u32[]{:S(2)}) copy-start(bf16[4,2,48,1024]{3,2,1,0:T(8,128)(2,1)S(1)} %collective-permute-done.15.refs_8_) | copy-start | bytes 2359300
  78.5 21.3 %collective-permute-start.14 = (bf16[4,2,48,1024]{3,2,1,0:T(8,128)(2,1)S(1)}, bf16[4,2,48,1024]{3,2,1,0:T(8,128)(2,1)}, u32[]{:S(2)}, u32[]{:S(2)}) collective-permute-start(bf16[4,2,48,1024]{3,2,1,0:T(8,128)(2,1)S(1)} %pad_maximum_fusion.1.refs_4_), channel_id=1, source_target_pairs={{96,0},{0,32},{32,64},{64,96},{97,1},{1,33},{33,65},{65,97},{98,2}... | collective-permute-start | bytes 2359304 | tf_op jit(solution)/shard_map/ppermute | solution.py:28
  79.6 37.5 %collective-permute-start.13 = (bf16[4,2,48,1024]{3,2,1,0:T(8,128)(2,1)S(1)}, bf16[4,2,48,1024]{3,2,1,0:T(8,128)(2,1)}, u32[]{:S(2)}, u32[]{:S(2)}) collective-permute-start(bf16[4,2,48,1024]{3,2,1,0:T(8,128)(2,1)S(1)} %pad_maximum_fusion.1.refs_4_), channel_id=1, source_target_pairs={{64,0},{96,32},{0,64},{32,96},{65,1},{97,33},{1,65},{33,97},{66,2}... | collective-permute-start | bytes 2359304 | tf_op jit(solution)/shard_map/ppermute | solution.py:28
  82.3 35.0 %collective-permute-start.12 = (bf16[4,2,48,1024]{3,2,1,0:T(8,128)(2,1)S(1)}, bf16[4,2,48,1024]{3,2,1,0:T(8,128)(2,1)}, u32[]{:S(2)}, u32[]{:S(2)}) collective-permute-start(bf16[4,2,48,1024]{3,2,1,0:T(8,128)(2,1)S(1)} %pad_maximum_fusion.1.refs_4_), channel_id=1, source_target_pairs={{32,0},{64,32},{96,64},{0,96},{33,1},{65,33},{97,65},{1,97},{34,2}... | collective-permute-start | bytes 2359304 | tf_op jit(solution)/shard_map/ppermute | solution.py:28
  83.7 33.9 %collective-permute-start.18 = (bf16[4,2,48,1024]{3,2,1,0:T(8,128)(2,1)S(1)}, bf16[4,2,48,1024]{3,2,1,0:T(8,128)(2,1)}, u32[]{:S(2)}, u32[]{:S(2)}) collective-permute-start(bf16[4,2,48,1024]{3,2,1,0:T(8,128)(2,1)S(1)} %collective-permute-done.6.refs_3_), channel_id=1, source_target_pairs={{0,1},{1,0},{2,3},{3,2},{4,5},{5,4},{6,7},{7,6},{8,9},{9,8},{10,11... | collective-permute-start | bytes 2359304 | tf_op jit(solution)/shard_map/ppermute | solution.py:36
  84.2 48.7 %collective-permute-start.17 = (bf16[4,2,48,1024]{3,2,1,0:T(8,128)(2,1)}, bf16[4,2,48,1024]{3,2,1,0:T(8,128)(2,1)}, u32[]{:S(2)}, u32[]{:S(2)}) collective-permute-start(bf16[4,2,48,1024]{3,2,1,0:T(8,128)(2,1)} %collective-permute-done.5.refs_2_), channel_id=1, source_target_pairs={{0,1},{1,0},{2,3},{3,2},{4,5},{5,4},{6,7},{7,6},{8,9},{9,8},{10,11... | collective-permute-start | bytes 2359304 | tf_op jit(solution)/shard_map/ppermute | solution.py:36
  99.9 33.0 %collective-permute-start.16 = (bf16[4,2,48,1024]{3,2,1,0:T(8,128)(2,1)}, bf16[4,2,48,1024]{3,2,1,0:T(8,128)(2,1)}, u32[]{:S(2)}, u32[]{:S(2)}) collective-permute-start(bf16[4,2,48,1024]{3,2,1,0:T(8,128)(2,1)} %collective-permute-done.4.refs_1_), channel_id=1, source_target_pairs={{0,1},{1,0},{2,3},{3,2},{4,5},{5,4},{6,7},{7,6},{8,9},{9,8},{10,11... | collective-permute-start | bytes 2359304 | tf_op jit(solution)/shard_map/ppermute | solution.py:36
  117.1 15.8 %collective-permute-start.22 = (bf16[4,2,48,1024]{3,2,1,0:T(8,128)(2,1)}, bf16[4,2,48,1024]{3,2,1,0:T(8,128)(2,1)}, u32[]{:S(2)}, u32[]{:S(2)}) collective-permute-start(bf16[4,2,48,1024]{3,2,1,0:T(8,128)(2,1)} %collective-permute-done.14.refs_7_), channel_id=1, source_target_pairs={{0,1},{1,0},{2,3},{3,2},{4,5},{5,4},{6,7},{7,6},{8,9},{9,8},{10,11... | collective-permute-start | bytes 2359304 | tf_op jit(solution)/shard_map/ppermute | solution.py:36
  117.3 15.6 %collective-permute-start.21 = (bf16[4,2,48,1024]{3,2,1,0:T(8,128)(2,1)}, bf16[4,2,48,1024]{3,2,1,0:T(8,128)(2,1)}, u32[]{:S(2)}, u32[]{:S(2)}) collective-permute-start(bf16[4,2,48,1024]{3,2,1,0:T(8,128)(2,1)} %collective-permute-done.13.refs_6_), channel_id=1, source_target_pairs={{0,1},{1,0},{2,3},{3,2},{4,5},{5,4},{6,7},{7,6},{8,9},{9,8},{10,11... | collective-permute-start | bytes 2359304 | tf_op jit(solution)/shard_map/ppermute | solution.py:36
  117.6 15.3 %collective-permute-start.20 = (bf16[4,2,48,1024]{3,2,1,0:T(8,128)(2,1)}, bf16[4,2,48,1024]{3,2,1,0:T(8,128)(2,1)}, u32[]{:S(2)}, u32[]{:S(2)}) collective-permute-start(bf16[4,2,48,1024]{3,2,1,0:T(8,128)(2,1)} %collective-permute-done.12.refs_5_), channel_id=1, source_target_pairs={{0,1},{1,0},{2,3},{3,2},{4,5},{5,4},{6,7},{7,6},{8,9},{9,8},{10,11... | collective-permute-start | bytes 2359304 | tf_op jit(solution)/shard_map/ppermute | solution.py:36
  119.2 12.9 %all-to-all-start = ((f32[16,1,2]{2,1,0:T(1,128)}), f32[16,1,2]{2,1,0:T(1,128)S(1)}, u32[]{:S(2)}, u32[]{:S(2)}) async-start(f32[16,1,2]{2,1,0:T(1,128)} %copy.24), calls=%async_computation | async-start | bytes 16384 | tf_op jit(solution)/shard_map/all_to_all | solution.py:40
  163.2 10.4 %all-to-all-start.1 = ((f32[8,19,128]{2,1,0:T(8,128)}), f32[8,19,128]{2,1,0:T(8,128)S(1)}, u32[]{:S(2)}, u32[]{:S(2)}) async-start(f32[8,19,128]{2,1,0:T(8,128)} %broadcast_in_dim.94), calls=%async_computation.1 | async-start | bytes 196608 | tf_op jit(solution)/shard_map/all_to_all | solution.py:40
  202.8 6.0 %collective-permute-start.31 = (bf16[2,768,1024]{2,1,0:T(8,128)(2,1)}, bf16[2,768,1024]{2,1,0:T(8,128)(2,1)}, u32[]{:S(2)}, u32[]{:S(2)}) collective-permute-start(bf16[2,768,1024]{2,1,0:T(8,128)(2,1)} %shard_map.108), channel_id=1, source_target_pairs={{0,1},{1,0},{2,3},{3,2},{4,5},{5,4},{6,7},{7,6},{8,9},{9,8},{10,11... | collective-permute-start | bytes 9437192 | tf_op jit(solution)/shard_map/ppermute | solution.py:36
  202.8 18.3 %collective-permute-start.23 = (bf16[2,768,1024]{2,1,0:T(8,128)(2,1)}, bf16[2,768,1024]{2,1,0:T(8,128)(2,1)S(1)}, u32[]{:S(2)}, u32[]{:S(2)}) collective-permute-start(bf16[2,768,1024]{2,1,0:T(8,128)(2,1)} %get-tuple-element.22), channel_id=1, source_target_pairs={{0,1},{1,0},{2,3},{3,2},{4,5},{5,4},{6,7},{7,6},{8,9},{9,8},{10,11... | collective-permute-start | bytes 9437192 | tf_op jit(solution)/shard_map/ppermute | solution.py:36
  216.8 37.9 %collective-permute-start.32 = (bf16[4,2,48,1024]{3,2,1,0:T(8,128)(2,1)}, bf16[4,2,48,1024]{3,2,1,0:T(8,128)(2,1)S(1)}, u32[]{:S(2)}, u32[]{:S(2)}) collective-permute-start(bf16[4,2,48,1024]{3,2,1,0:T(8,128)(2,1)} %get-tuple-element.28), channel_id=1, source_target_pairs={{0,32},{32,64},{64,96},{96,0},{1,33},{33,65},{65,97},{97,1},{2,34}... | collective-permute-start | bytes 2359304 | tf_op jit(solution)/shard_map/ppermute | solution.py:32
  217.6 39.1 %collective-permute-start.33 = (bf16[4,2,48,1024]{3,2,1,0:T(8,128)(2,1)}, bf16[4,2,48,1024]{3,2,1,0:T(8,128)(2,1)S(1)}, u32[]{:S(2)}, u32[]{:S(2)}) collective-permute-start(bf16[4,2,48,1024]{3,2,1,0:T(8,128)(2,1)} %get-tuple-element.29), channel_id=1, source_target_pairs={{0,96},{32,0},{64,32},{96,64},{1,97},{33,1},{65,33},{97,65},{2,98}... | collective-permute-start | bytes 2359304 | tf_op jit(solution)/shard_map/ppermute | solution.py:32
  220.4 36.3 %collective-permute-start.34 = (bf16[4,2,48,1024]{3,2,1,0:T(8,128)(2,1)}, bf16[4,2,48,1024]{3,2,1,0:T(8,128)(2,1)S(1)}, u32[]{:S(2)}, u32[]{:S(2)}) collective-permute-start(bf16[4,2,48,1024]{3,2,1,0:T(8,128)(2,1)} %get-tuple-element.30), channel_id=1, source_target_pairs={{0,64},{32,96},{64,0},{96,32},{1,65},{33,97},{65,1},{97,33},{2,66}... | collective-permute-start | bytes 2359304 | tf_op jit(solution)/shard_map/ppermute | solution.py:32
  230.7 29.9 %collective-permute-start.24 = (bf16[4,2,48,1024]{3,2,1,0:T(8,128)(2,1)}, bf16[4,2,48,1024]{3,2,1,0:T(8,128)(2,1)S(1)}, u32[]{:S(2)}, u32[]{:S(2)}) collective-permute-start(bf16[4,2,48,1024]{3,2,1,0:T(8,128)(2,1)} %get-tuple-element.24), channel_id=1, source_target_pairs={{0,8},{8,16},{16,24},{24,0},{1,9},{9,17},{17,25},{25,1},{2,10},{10... | collective-permute-start | bytes 2359304 | tf_op jit(solution)/shard_map/ppermute | solution.py:32
  231.2 35.1 %collective-permute-start.25 = (bf16[4,2,48,1024]{3,2,1,0:T(8,128)(2,1)}, bf16[4,2,48,1024]{3,2,1,0:T(8,128)(2,1)S(1)}, u32[]{:S(2)}, u32[]{:S(2)}) collective-permute-start(bf16[4,2,48,1024]{3,2,1,0:T(8,128)(2,1)} %get-tuple-element.25), channel_id=1, source_target_pairs={{0,24},{8,0},{16,8},{24,16},{1,25},{9,1},{17,9},{25,17},{2,26},{10... | collective-permute-start | bytes 2359304 | tf_op jit(solution)/shard_map/ppermute | solution.py:32
  254.7 17.0 %collective-permute-start.26 = (bf16[4,2,48,1024]{3,2,1,0:T(8,128)(2,1)}, bf16[4,2,48,1024]{3,2,1,0:T(8,128)(2,1)S(1)}, u32[]{:S(2)}, u32[]{:S(2)}) collective-permute-start(bf16[4,2,48,1024]{3,2,1,0:T(8,128)(2,1)} %get-tuple-element.26), channel_id=1, source_target_pairs={{0,16},{8,24},{16,0},{24,8},{1,17},{9,25},{17,1},{25,9},{2,18},{10... | collective-permute-start | bytes 2359304 | tf_op jit(solution)/shard_map/ppermute | solution.py:32
  257.4 19.3 %collective-permute-start.35 = (bf16[2,48,1024]{2,1,0:T(8,128)(2,1)S(1)}, bf16[2,48,1024]{2,1,0:T(8,128)(2,1)S(1)}, u32[]{:S(2)}, u32[]{:S(2)}) collective-permute-start(bf16[2,48,1024]{2,1,0:T(8,128)(2,1)S(1)} %get-tuple-element.36), channel_id=1, source_target_pairs={{0,8},{8,16},{16,24},{24,0},{1,9},{9,17},{17,25},{25,1},{2,10},{10... | collective-permute-start | bytes 589832 | tf_op jit(solution)/shard_map/ppermute | solution.py:32
  258.1 21.2 %collective-permute-start.37 = (bf16[2,48,1024]{2,1,0:T(8,128)(2,1)S(1)}, bf16[2,48,1024]{2,1,0:T(8,128)(2,1)S(1)}, u32[]{:S(2)}, u32[]{:S(2)}) collective-permute-start(bf16[2,48,1024]{2,1,0:T(8,128)(2,1)S(1)} %get-tuple-element.37), channel_id=1, source_target_pairs={{0,16},{8,24},{16,0},{24,8},{1,17},{9,25},{17,1},{25,9},{2,18},{10... | collective-permute-start | bytes 589832 | tf_op jit(solution)/shard_map/ppermute | solution.py:32
  260.6 18.7 %collective-permute-start.36 = (bf16[2,48,1024]{2,1,0:T(8,128)(2,1)S(1)}, bf16[2,48,1024]{2,1,0:T(8,128)(2,1)S(1)}, u32[]{:S(2)}, u32[]{:S(2)}) collective-permute-start(bf16[2,48,1024]{2,1,0:T(8,128)(2,1)S(1)} %get-tuple-element.38), channel_id=1, source_target_pairs={{0,24},{8,0},{16,8},{24,16},{1,25},{9,1},{17,9},{25,17},{2,26},{10... | collective-permute-start | bytes 589832 | tf_op jit(solution)/shard_map/ppermute | solution.py:32
  272.4 9.7 %collective-permute-start.27 = (bf16[2,48,1024]{2,1,0:T(8,128)(2,1)S(1)}, bf16[2,48,1024]{2,1,0:T(8,128)(2,1)S(1)}, u32[]{:S(2)}, u32[]{:S(2)}) collective-permute-start(bf16[2,48,1024]{2,1,0:T(8,128)(2,1)S(1)} %get-tuple-element.33), channel_id=1, source_target_pairs={{0,32},{32,64},{64,96},{96,0},{1,33},{33,65},{65,97},{97,1},{2,34}... | collective-permute-start | bytes 589832 | tf_op jit(solution)/shard_map/ppermute | solution.py:32
  274.5 7.8 %collective-permute-start.29 = (bf16[2,48,1024]{2,1,0:T(8,128)(2,1)S(1)}, bf16[2,48,1024]{2,1,0:T(8,128)(2,1)S(1)}, u32[]{:S(2)}, u32[]{:S(2)}) collective-permute-start(bf16[2,48,1024]{2,1,0:T(8,128)(2,1)S(1)} %get-tuple-element.34), channel_id=1, source_target_pairs={{0,64},{32,96},{64,0},{96,32},{1,65},{33,97},{65,1},{97,33},{2,66}... | collective-permute-start | bytes 589832 | tf_op jit(solution)/shard_map/ppermute | solution.py:32
  276.7 5.7 %collective-permute-start.28 = (bf16[2,48,1024]{2,1,0:T(8,128)(2,1)S(1)}, bf16[2,48,1024]{2,1,0:T(8,128)(2,1)S(1)}, u32[]{:S(2)}, u32[]{:S(2)}) collective-permute-start(bf16[2,48,1024]{2,1,0:T(8,128)(2,1)S(1)} %get-tuple-element.35), channel_id=1, source_target_pairs={{0,96},{32,0},{64,32},{96,64},{1,97},{33,1},{65,33},{97,65},{2,98}... | collective-permute-start | bytes 589832 | tf_op jit(solution)/shard_map/ppermute | solution.py:32
  279.4 4.7 %collective-permute-start.38 = (bf16[48,1024]{1,0:T(8,128)(2,1)S(1)}, bf16[48,1024]{1,0:T(8,128)(2,1)S(1)}, u32[]{:S(2)}, u32[]{:S(2)}) collective-permute-start(bf16[48,1024]{1,0:T(8,128)(2,1)S(1)} %get-tuple-element.39), channel_id=1, source_target_pairs={{0,6},{2,0},{4,2},{6,4},{1,7},{3,1},{5,3},{7,5},{8,14},{10,8},{12,... | collective-permute-start | bytes 294920 | tf_op jit(solution)/shard_map/ppermute | solution.py:32
  280.6 6.1 %collective-permute-start.39 = (bf16[48,1024]{1,0:T(8,128)(2,1)S(1)}, bf16[48,1024]{1,0:T(8,128)(2,1)S(1)}, u32[]{:S(2)}, u32[]{:S(2)}) collective-permute-start(bf16[48,1024]{1,0:T(8,128)(2,1)S(1)} %get-tuple-element.40), channel_id=1, source_target_pairs={{0,4},{2,6},{4,0},{6,2},{1,5},{3,7},{5,1},{7,3},{8,12},{10,14},{12... | collective-permute-start | bytes 294920 | tf_op jit(solution)/shard_map/ppermute | solution.py:32
  282.6 5.9 %collective-permute-start.30 = (bf16[48,1024]{1,0:T(8,128)(2,1)S(1)}, bf16[48,1024]{1,0:T(8,128)(2,1)S(1)}, u32[]{:S(2)}, u32[]{:S(2)}) collective-permute-start(bf16[48,1024]{1,0:T(8,128)(2,1)S(1)} %slice_bitcast_fusion.10), channel_id=1, source_target_pairs={{0,2},{2,4},{4,6},{6,0},{1,3},{3,5},{5,7},{7,1},{8,10},{10,12},{12... | collective-permute-start | bytes 294920 | tf_op jit(solution)/shard_map/ppermute | solution.py:32
  (6 other events, 129.4 us)
